TPU v7x, 32 devices: a whole 2x2x4 slice. The times are simulated.
32 devices in a mesh: dp: 8 (over z, y), fsdp: 4 (over x, core).
Axes of the slice: x: 2, y: 2, z: 4, core: 2. Of those that a mesh axis runs over, the one named last changes fastest.
Arguments:
- tokens: int32 [96, 512], P(('dp', 'fsdp'))
- grad_y: bfloat16 [96, 512, 1280], P(('dp', 'fsdp'))
- embedding: bfloat16 [33, 1280], P(None, 'fsdp')
- ln1_gain: bfloat16 [1280], P('fsdp')
- ln1_bias: bfloat16 [1280], P('fsdp')
- w_qkv: bfloat16 [1280, 3840], P('fsdp')
- b_qkv: bfloat16 [3840], P('fsdp')
- w_out: bfloat16 [1280, 1280], P('fsdp')
- b_out: bfloat16 [1280], P('fsdp')
- ln2_gain: bfloat16 [1280], P('fsdp')
- ln2_bias: bfloat16 [1280], P('fsdp')
- w_fc1: bfloat16 [1280, 5120], P('fsdp')
- b_fc1: bfloat16 [5120], P('fsdp')
- w_fc2: bfloat16 [5120, 1280], P('fsdp')
- b_fc2: bfloat16 [1280], P('fsdp')
Outputs:
- output 1: bfloat16 [96, 512, 1280], P(('dp', 'fsdp'))
- output 2: float32 [33, 1280], P(None, 'fsdp')
- output 3: float32 [1280], P('fsdp')
- output 4: float32 [1280], P('fsdp')
- output 5: float32 [1280, 3840], P('fsdp')
- output 6: float32 [3840], P('fsdp')
- output 7: float32 [1280, 1280], P('fsdp')
- output 8: float32 [1280], P('fsdp')
- output 9: float32 [1280], P('fsdp')
- output 10: float32 [1280], P('fsdp')
- output 11: float32 [1280, 5120], P('fsdp')
- output 12: float32 [5120], P('fsdp')
- output 13: float32 [5120, 1280], P('fsdp')
- output 14: float32 [1280], P('fsdp')
All inputs are finite; a program needn't handle non-finite values.
Results may differ from a plain program's by a relative error of at most 0.0115641.
Values are sent between devices in bfloat16 or wider.
A program may use at most 1 GiB of HBM per device.

v0:
```python
import functools
import jax
import jax.numpy as jnp
from jax import lax
from jax.sharding import PartitionSpec as P

HEAD_DIM = 64
MASK_ID = 32
PAD_ID = 1
MASK_RATIO = 0.15 * 0.8
LN_EPS = 1e-5
ROPE_BASE = 10000.0


def f32_einsum(form, lhs, rhs):
    return jnp.einsum(form, lhs, rhs, preferred_element_type=jnp.float32)


def norm_fwd(x_val, gain, bias):
    centered = x_val - jnp.mean(x_val, axis=-1, keepdims=True)
    inv_std = lax.rsqrt(jnp.mean(centered * centered, axis=-1, keepdims=True) + LN_EPS)
    x_hat = centered * inv_std
    return x_hat * gain.astype(jnp.float32) + bias.astype(jnp.float32), x_hat, inv_std


def norm_bwd(d_out, x_hat, inv_std, gain):
    d_hat = d_out * gain.astype(jnp.float32)
    d_x = inv_std * (d_hat - jnp.mean(d_hat, axis=-1, keepdims=True)
                     - x_hat * jnp.mean(d_hat * x_hat, axis=-1, keepdims=True))
    return d_x, jnp.sum(d_out * x_hat, axis=(0, 1)), jnp.sum(d_out, axis=(0, 1))


def rope_tables(seq_len):
    inv_freq = 1.0 / (ROPE_BASE ** (jnp.arange(0, HEAD_DIM, 2, dtype=jnp.float32) / HEAD_DIM))
    angles = jnp.arange(seq_len, dtype=jnp.float32)[:, None] * inv_freq[None, :]
    return jnp.cos(angles)[:, None, :], jnp.sin(angles)[:, None, :]


def rotate(x_val, cos_tab, sin_tab):
    half_dim = x_val.shape[-1] // 2
    low_half = x_val[..., :half_dim]
    high_half = x_val[..., half_dim:]
    return jnp.concatenate([low_half * cos_tab - high_half * sin_tab, high_half * cos_tab + low_half * sin_tab], axis=-1)


def layer_step(tokens, grad_y, weights):
    (embedding, ln1_gain, ln1_bias, w_qkv, b_qkv, w_out, b_out,
     ln2_gain, ln2_bias, w_fc1, b_fc1, w_fc2, b_fc2) = weights
    batch_rows, seq_len = tokens.shape
    vocab_size, model_dim = embedding.shape
    num_heads = model_dim // HEAD_DIM
    one_hot = tokens[:, :, None] == jnp.arange(vocab_size)[None, None, :]
    is_mask = tokens == MASK_ID
    is_pad = tokens == PAD_ID
    mask_count = jnp.sum(is_mask, axis=1).astype(jnp.float32)
    real_count = jnp.sum(jnp.logical_not(is_pad), axis=1).astype(jnp.float32)
    factor = (1.0 - MASK_RATIO) / (1.0 - mask_count / real_count)
    keep_scale = jnp.where(is_mask | is_pad, 0.0, factor[:, None])[:, :, None]
    looked_up = f32_einsum('blv,vd->bld', one_hot.astype(jnp.bfloat16), embedding)
    x_res = (looked_up * keep_scale).astype(jnp.bfloat16).astype(jnp.float32)
    norm_one, hat_one, inv_one = norm_fwd(x_res, ln1_gain, ln1_bias)
    h_one = norm_one.astype(jnp.bfloat16)
    qkv_proj = f32_einsum('bld,de->ble', h_one, w_qkv) + b_qkv.astype(jnp.float32)
    qkv_proj = qkv_proj.reshape(batch_rows, seq_len, 3, num_heads, HEAD_DIM)
    cos_tab, sin_tab = rope_tables(seq_len)
    queries = rotate(qkv_proj[:, :, 0] * HEAD_DIM ** -0.5, cos_tab, sin_tab).astype(jnp.bfloat16)
    key_rows = rotate(qkv_proj[:, :, 1], cos_tab, sin_tab).astype(jnp.bfloat16)
    values = qkv_proj[:, :, 2].astype(jnp.bfloat16)
    scores = f32_einsum('bqhd,bkhd->bhqk', queries, key_rows)
    scores = jnp.where(is_pad[:, None, None, :], -1e30, scores)
    attn_prob = jax.nn.softmax(scores, axis=-1)
    prob_b16 = attn_prob.astype(jnp.bfloat16)
    context = f32_einsum('bhqk,bkhd->bqhd', prob_b16, values).astype(jnp.bfloat16)
    context = context.reshape(batch_rows, seq_len, model_dim)
    x_mid = x_res + f32_einsum('bld,de->ble', context, w_out) + b_out.astype(jnp.float32)
    norm_two, hat_two, inv_two = norm_fwd(x_mid, ln2_gain, ln2_bias)
    h_two = norm_two.astype(jnp.bfloat16)
    pre_act = f32_einsum('bld,df->blf', h_two, w_fc1) + b_fc1.astype(jnp.float32)
    hidden_act, gelu_pull = jax.vjp(functools.partial(jax.nn.gelu, approximate=False), pre_act)
    act_b16 = hidden_act.astype(jnp.bfloat16)
    hidden = (x_mid + f32_einsum('blf,fd->bld', act_b16, w_fc2) + b_fc2.astype(jnp.float32)).astype(jnp.bfloat16)

    grad_res = grad_y.astype(jnp.float32)
    g_b_fc2 = jnp.sum(grad_res, axis=(0, 1))
    g_w_fc2 = f32_einsum('blf,bld->fd', act_b16, grad_y)
    d_pre = gelu_pull(f32_einsum('bld,fd->blf', grad_y, w_fc2))[0]
    g_b_fc1 = jnp.sum(d_pre, axis=(0, 1))
    d_pre = d_pre.astype(jnp.bfloat16)
    g_w_fc1 = f32_einsum('bld,blf->df', h_two, d_pre)
    d_two, g_ln2_gain, g_ln2_bias = norm_bwd(f32_einsum('blf,df->bld', d_pre, w_fc1), hat_two, inv_two, ln2_gain)
    d_mid = grad_res + d_two
    g_b_out = jnp.sum(d_mid, axis=(0, 1))
    d_mid_b16 = d_mid.astype(jnp.bfloat16)
    g_w_out = f32_einsum('bld,ble->de', context, d_mid_b16)
    d_ctx = f32_einsum('ble,de->bld', d_mid_b16, w_out).astype(jnp.bfloat16)
    d_ctx = d_ctx.reshape(batch_rows, seq_len, num_heads, HEAD_DIM)
    d_prob = f32_einsum('bqhd,bkhd->bhqk', d_ctx, values)
    d_val = f32_einsum('bhqk,bqhd->bkhd', prob_b16, d_ctx)
    d_scores = attn_prob * (d_prob - jnp.sum(d_prob * attn_prob, axis=-1, keepdims=True))
    d_scores = d_scores.astype(jnp.bfloat16)
    d_query = rotate(f32_einsum('bhqk,bkhd->bqhd', d_scores, key_rows), cos_tab, -sin_tab) * HEAD_DIM ** -0.5
    d_key = rotate(f32_einsum('bhqk,bqhd->bkhd', d_scores, queries), cos_tab, -sin_tab)
    d_qkv = jnp.stack([d_query, d_key, d_val], axis=2).reshape(batch_rows, seq_len, 3 * model_dim)
    g_b_qkv = jnp.sum(d_qkv, axis=(0, 1))
    d_qkv = d_qkv.astype(jnp.bfloat16)
    g_w_qkv = f32_einsum('bld,ble->de', h_one, d_qkv)
    d_one, g_ln1_gain, g_ln1_bias = norm_bwd(f32_einsum('ble,de->bld', d_qkv, w_qkv), hat_one, inv_one, ln1_gain)
    d_in = d_mid + d_one
    g_embedding = f32_einsum('blv,bld->vd', one_hot.astype(jnp.float32), d_in * keep_scale)
    full_grads = (g_embedding, g_ln1_gain, g_ln1_bias, g_w_qkv, g_b_qkv, g_w_out, g_b_out,
                  g_ln2_gain, g_ln2_bias, g_w_fc1, g_b_fc1, g_w_fc2, g_b_fc2)
    return hidden, full_grads


def solution(mesh):
    row_spec = P(('dp', 'fsdp'), None)
    act_spec = P(('dp', 'fsdp'), None, None)
    param_specs = (P(None, 'fsdp'),) + (P('fsdp'),) * 12

    def local_step(tokens, grad_y, *shards):
        full_params = [lax.all_gather(shards[0], 'fsdp', axis=1, tiled=True)]
        full_params += [lax.all_gather(shard, 'fsdp', axis=0, tiled=True) for shard in shards[1:]]
        hidden, full_grads = layer_step(tokens, grad_y, full_params)
        grad_parts = [lax.psum(lax.psum_scatter(full_grads[0], 'fsdp', scatter_dimension=1, tiled=True), 'dp')]
        grad_parts += [lax.psum(lax.psum_scatter(full_grad, 'fsdp', scatter_dimension=0, tiled=True), 'dp')
                       for full_grad in full_grads[1:]]
        return (hidden,) + tuple(grad_parts)

    return jax.shard_map(local_step, mesh=mesh, in_specs=(row_spec, act_spec) + param_specs,
                         out_specs=(act_spec,) + param_specs, check_vma=False)
```

profile of v0, /device:TPU:0, one launch (start us, length us, event | category | flops | bytes accessed | tf_op | source)
XLA Modules:
  0.0 1890.1 jit_solution(9459882133817304712)
XLA Ops:
  13.9 14.2 all-reduce.18
  28.3 6.2 all-gather
  42.0 5.7 all-gather.1
  48.3 31.5 %all-gather.7.cloned.1.call-done = bf16[1280,3840]{1,0:T(8,128)(2,1)} async-done(((bf16[320,3840]{1,0:T(8,128)(2,1)}), bf16[1280,3840]{1,0:T(8,128)(2,1)}) %all-gather.7.cloned.1.call-update) | async-done | bytes 9830416 | tf_op jit(solution)/shard_map/all_gather | solution.py:122
  79.8 23.9 %broadcast_add_fusion = f32[3,512,3840]{2,1,0:T(8,128)} fusion(f32[3840]{0:T(1024)S(1)} %convert_element_type.111, bf16[1280,3840]{1,0:T(8,128)(2,1)} %all-gather.7.cloned.1.call-done, bf16[3,512,1280]{2,1,0:T(8,128)(2,1)} %copy-done.5, f32[1280]{0:T(1024)S(1)} %convert_element_type.109, f32[1280]{0:T(1024)S(1)} %convert_element_type.108, ...), kind=kOutput, calls=%fused_computation.49 | convolution fusion | flops 15117189120 | bytes 37393408 | tf_op jit(solution)/shard_map/bld,de->ble/dot_general | solution.py:16
  103.7 24.7 %copy.61 = f32[3,512,3840]{1,2,0:T(8,128)} copy(f32[3,512,3840]{2,1,0:T(8,128)} %broadcast_add_fusion) | data formatting | bytes 47185920 | tf_op jit(solution)/shard_map/add | solution.py:63
  128.4 14.6 fusion.99
  143.0 14.9 copy_bitcast_fusion
  157.9 8.7 subtract_convert_fusion.1
  166.6 30.1 %fusion.101 = (f32[3,20,512]{2,1,0:T(8,128)S(1)}, f32[3,20,512,512]{2,3,1,0:T(8,128)}) fusion(pred[3,512]{1,0:T(4,128)(4,1)S(1)} %get-tuple-element.59, bf16[3,512,20,32]{1,3,2,0:T(8,128)(2,1)S(1)} %get-tuple-element.73, bf16[3,512,20,32]{1,3,2,0:T(8,128)(2,1)} %get-tuple-element.74, bf16[3,512,20,32]{1,3,2,0:T(8,128)(2,1)} %get-tuple-element.67, ...), kind=kOutput, calls=%fused_computation.156 | convolution fusion | flops 2076180992 | bytes 70903296 | tf_op jit(solution)/shard_map/sub | solution.py:71
  196.7 28.9 %fusion.71 = bf16[3,20,64,512]{3,2,1,0:T(8,128)(2,1)} fusion(f32[3,20,512,512]{2,3,1,0:T(8,128)} %get-tuple-element.85, f32[3,20,512]{2,1,0:T(8,128)S(1)} %get-tuple-element.84, f32[3,512,3,20,64]{1,4,3,2,0:T(8,128)} %bitcast.106), kind=kOutput, calls=%fused_computation.119 | convolution fusion | flops 2046689280 | bytes 70901760 | tf_op jit(solution)/shard_map/bhqk,bkhd->bqhd/dot_general | solution.py:16
  225.7 9.7 fusion.102
  235.4 3.1 copy-done
  239.6 45.5 %fusion.53 = (u8[512,5120]{1,0:T(8,128)(4,1)S(1)}, u8[512,5120]{1,0:T(8,128)(4,1)}, f32[3,512,5120]{2,1,0:T(8,128)}) fusion(f32[5120]{0:T(1024)S(1)} %bitcast.117, bf16[1280,5120]{1,0:T(8,128)(2,1)} %all-gather.11.cloned.1.call-done, f32[3,512,1280]{2,1,0:T(8,128)} %copy-done, f32[1280]{0:T(1024)S(1)} %copy-done.27, f32[1280]{0:T(1024)S(1)} %copy-done.18, ...), kind=kOutput, calls=%fused_computation.91 | convolution fusion | flops 20247347200 | bytes 57714688 | tf_op jit(solution)/shard_map/bld,df->blf/dot_general | solution.py:16
  285.0 75.5 %multiply_convert_fusion.1 = (bf16[3,512,5120]{2,1,0:T(8,128)(2,1)}, f32[3,512,5120]{2,1,0:T(8,128)}) fusion(f32[3,512,5120]{2,1,0:T(8,128)} %get-tuple-element.88, f32[5120]{0:T(1024)S(1)} %bitcast.118, u8[512,5120]{1,0:T(8,128)(4,1)} %get-tuple-element.15, u8[512,5120]{1,0:T(8,128)(4,1)S(1)} %get-tuple-element.14), kind=kLoop, calls=%fused_computation.14 | loop fusion | flops 558366720 | bytes 83906560 | tf_op jit(solution)/shard_map/convert_element_type | solution.py:80
  360.5 43.8 %fusion.103 = (f32[5120]{0:T(1024)}, bf16[3,512,5120]{2,1,0:T(8,128)(2,1)}) fusion(f32[3,512,5120]{2,1,0:T(8,128)} %get-tuple-element.55, bf16[3,512,1280]{2,1,0:T(8,128)(2,1)} %param.16, bf16[5120,1280]{1,0:T(8,128)(2,1)} %all-gather.13.cloned.1.call-done, f32[3,512,5120]{2,1,0:T(8,128)} %get-tuple-element.88, f32[5120]{0:T(1024)S(1)} %bitcast.119), kind=kOutput, calls=%fused_computation.158 | convolution fusion | flops 20258484224 | bytes 95723520 | tf_op jit(solution)/shard_map/bld,fd->blf/dot_general | solution.py:16
  404.3 31.1 %multiply_reduce_fusion.1 = (f32[1280]{0:T(1024)}, f32[3,512]{1,0:T(4,128)S(1)}, f32[3,512]{1,0:T(4,128)S(1)}, f32[1280]{0:T(1024)}, f32[3,512,1280]{2,1,0:T(8,128)}) fusion(f32[3,512,1280]{2,1,0:T(8,128)} %copy-done, f32[3,512]{1,0:T(4,128)S(1)} %add_rsqrt_fusion, f32[3,512]{1,0:T(4,128)S(1)} %broadcast_multiply_fusion.4, f32[1280]{0:T(1024)S(1)} %copy-done.18, ...), kind=kOutput, calls=%fused_computation.81 | convolution fusion | flops 20150345728 | bytes 44604416 | tf_op jit(solution)/shard_map/blf,df->bld/dot_general | solution.py:16
  435.5 9.1 fusion.97
  444.6 3.1 copy-done.2
  447.7 7.2 convolution_convert_fusion
  454.8 6.3 copy.67
  461.2 44.5 %multiply_reduce_fusion = (f32[3,20,512]{2,1,0:T(8,128)S(1)}, f32[3,20,512,512]{2,3,1,0:T(8,128)}) fusion(f32[3,20,512,512]{2,3,1,0:T(8,128)} %get-tuple-element.85, f32[3,20,512]{2,1,0:T(8,128)S(1)} %copy-done.12, bf16[3,512,20,64]{1,3,2,0:T(8,128)(2,1)} %bitcast.114, f32[3,512,3,20,64]{1,4,3,2,0:T(8,128)} %bitcast.107), kind=kOutput, calls=%fused_computation.2 | convolution fusion | flops 2060421120 | bytes 133939200 | tf_op jit(solution)/shard_map/bqhd,bkhd->bhqk/dot_general | solution.py:16
  505.7 50.2 %multiply_convert_fusion = bf16[3,20,512,512]{2,3,1,0:T(8,128)(2,1)} fusion(f32[3,20,512,512]{2,3,1,0:T(8,128)} %get-tuple-element.91, f32[3,20,512]{2,1,0:T(8,128)S(1)} %get-tuple-element.90, f32[3,20,512,512]{2,3,1,0:T(8,128)} %get-tuple-element.85, f32[3,20,512]{2,1,0:T(8,128)S(1)} %copy-done.12), kind=kLoop, calls=%fused_computation.1 | loop fusion | flops 62914560 | bytes 157532160 | tf_op jit(solution)/shard_map/convert_element_type | solution.py:100
  555.9 18.8 convolution_bitcast_fusion.4
  574.6 19.2 %convolution_bitcast_fusion.5 = f32[3,512,20,64]{1,3,2,0:T(8,128)} fusion(bf16[3,20,512,512]{2,3,1,0:T(8,128)(2,1)} %multiply_convert_fusion, bf16[3,512,20,32]{1,3,2,0:T(8,128)(2,1)S(1)} %copy-done.4, bf16[3,512,20,32]{1,3,2,0:T(8,128)(2,1)} %get-tuple-element.74), kind=kOutput, calls=%fused_computation.118 | convolution fusion | flops 2021130240 | bytes 43253760 | tf_op jit(solution)/shard_map/bhqk,bkhd->bqhd/dot_general | solution.py:16
  593.8 11.0 convolution_bitcast_fusion.3
  604.9 7.1 subtract_bitcast_fusion
  612.1 5.6 maximum_multiply_fusion
  617.6 4.2 maximum_bitcast_fusion
  621.8 27.9 %fusion.68 = f32[3,512,1,20,64]{1,4,3,0,2:T(8,128)} fusion(bf16[3,512,20,64]{1,3,2,0:T(8,128)(2,1)} %bitcast.115, f32[3,20,512,512]{2,3,1,0:T(8,128)} %get-tuple-element.85, f32[3,20,512]{2,1,0:T(8,128)S(1)} %copy-done.12), kind=kOutput, calls=%fused_computation.116 | convolution fusion | flops 2044723200 | bytes 74833920 | tf_op jit(solution)/shard_map/bhqk,bqhd->bkhd/dot_general | solution.py:16
  649.7 9.4 fusion.15
  661.0 4.3 copy-done.1
  665.4 21.7 %convolution_bitcast_fusion.2 = f32[1280,3840]{1,0:T(8,128)} fusion(bf16[3,512,3840]{1,2,0:T(8,128)(2,1)S(1)} %bitcast.108, bf16[3,512,1280]{2,1,0:T(8,128)(2,1)S(1)} %copy-done.6, f32[1280]{0:T(1024)S(1)} %copy-done.26, f32[1280]{0:T(1024)S(1)} %copy-done.24, f32[3,512]{1,0:T(4,128)S(1)} %copy-done.33, f32[3,512]{1,0:T(4,128)S(1)} %copy-done.17), kind=kOutput, calls=%fused_computation.34 | convolution fusion | flops 15111290880 | bytes 35411968 | tf_op jit(solution)/shard_map/bld,ble->de/dot_general | solution.py:16
  687.8 30.4 %convolution_bitcast_fusion.1 = f32[1280,5120]{1,0:T(8,128)} fusion(bf16[3,512,5120]{2,1,0:T(8,128)(2,1)} %get-tuple-element.94, f32[3,512,1280]{2,1,0:T(8,128)} %copy-done, f32[1280]{0:T(1024)S(1)} %copy-done.28, f32[1280]{0:T(1024)S(1)} %copy-done.19, f32[3,512]{1,0:T(4,128)S(1)} %copy-done.21, f32[3,512]{1,0:T(4,128)S(1)} %copy-done.15), kind=kOutput, calls=%fused_computation.33 | convolution fusion | flops 20142489600 | bytes 49829888 | tf_op jit(solution)/shard_map/bld,blf->df/dot_general | solution.py:16
  718.3 28.2 %convolution_bitcast_fusion = f32[5120,1280]{1,0:T(8,128)} fusion(bf16[3,512,5120]{2,1,0:T(8,128)(2,1)} %get-tuple-element.54, bf16[3,512,1280]{2,1,0:T(8,128)(2,1)} %param.16), kind=kOutput, calls=%fused_computation.32 | convolution fusion | flops 20132659200 | bytes 45875200 | tf_op jit(solution)/shard_map/blf,bld->fd/dot_general | solution.py:16
  746.6 9.6 fusion.14
  756.9 25.6 %fusion.44 = (f32[1280]{0:T(1024)}, f32[3,512]{1,0:T(4,128)S(1)}, f32[3,512]{1,0:T(4,128)S(1)}, f32[1280]{0:T(1024)}, f32[3,512,1280]{2,1,0:T(8,128)}) fusion(bf16[3,512,1280]{2,1,0:T(8,128)(2,1)} %copy-done.5, f32[3,512]{1,0:T(4,128)S(1)} %copy-done.33, f32[3,512]{1,0:T(4,128)S(1)} %copy-done.17, f32[1280]{0:T(1024)S(1)} %copy-done.24, ...), kind=kOutput, calls=%fused_computation.72 | convolution fusion | flops 15119150080 | bytes 33463296 | tf_op jit(solution)/shard_map/ble,de->bld/dot_general | solution.py:16
  782.6 10.0 fusion.74
  792.6 36.8 %reduce-scatter.8.cloned.1.call-done = f32[320,3840]{1,0:T(8,128)} async-done(((f32[1280,3840]{1,0:T(8,128)}), f32[320,3840]{1,0:T(8,128)}) %reduce-scatter.8.cloned.1.call-update) | async-done | bytes 4915216 | tf_op jit(solution)/shard_map/reduce_scatter | solution.py:125
  829.5 191.5 %reduce-scatter.12.cloned.1.call-done = f32[320,5120]{1,0:T(8,128)} async-done(((f32[1280,5120]{1,0:T(8,128)}), f32[320,5120]{1,0:T(8,128)}) %reduce-scatter.12.cloned.1.call-update) | async-done | bytes 6553616 | tf_op jit(solution)/shard_map/reduce_scatter | solution.py:125
  1021.0 191.5 %reduce-scatter.14.cloned.1.call-done = f32[1280,1280]{1,0:T(8,128)} async-done(((f32[5120,1280]{1,0:T(8,128)}), f32[1280,1280]{1,0:T(8,128)}) %reduce-scatter.14.cloned.1.call-update) | async-done | bytes 6553616 | tf_op jit(solution)/shard_map/reduce_scatter | solution.py:125
  1214.4 28.5 %add_convert_fusion = bf16[3,512,1280]{2,1,0:T(8,128)(2,1)} fusion(f32[3,512,1280]{2,1,0:T(8,128)} %copy-done, bf16[3,512,5120]{2,1,0:T(8,128)(2,1)} %get-tuple-element.54, bf16[5120,1280]{1,0:T(8,128)(2,1)} %all-gather.13.cloned.1.call-done, f32[1280]{0:T(1024)S(1)} %convert_element_type.122), kind=kOutput, calls=%fused_computation.85 | convolution fusion | flops 20138557440 | bytes 40637440 | tf_op jit(solution)/shard_map/blf,fd->bld/dot_general | solution.py:16
  1242.9 4.3 all-reduce.24.cloned.1.call-done
  1253.4 20.8 %reduce-scatter.16.cloned.1.call-done = f32[320,33]{1,0:T(8,128)} async-done(((f32[1280,33]{1,0:T(8,128)}), f32[320,33]{1,0:T(8,128)}) %reduce-scatter.16.cloned.1.call-update) | async-done | bytes 42256
  1275.2 41.4 %all-reduce.15 = (f32[33,320]{1,0:T(8,128)}, f32[320]{0:T(512)}, f32[320]{0:T(512)}, f32[960]{0:T(1024)}, f32[320]{0:T(512)}, /*index=5*/f32[320]{0:T(512)}, f32[320]{0:T(512)}, f32[1280]{0:T(1024)}, f32[320]{0:T(512)}) all-reduce(f32[33,320]{1,0:T(8,128)S(1)} %copy.88, ...), channel_id=1, replica_groups=mesh['dp'=8,'fsdp'=4] {'dp'}, use_global_device_ids=true, to_apply=%region_14.15 | all-reduce | flops 14720 | bytes 117760 | tf_op jit(solution)/shard_map/psum | solution.py:124
  1316.6 552.5 %all-reduce.22.cloned.1.call-done = (f32[320,3840]{1,0:T(8,128)}, f32[320,1280]{1,0:T(8,128)}, f32[320,5120]{1,0:T(8,128)}, f32[1280,1280]{1,0:T(8,128)}) async-done(((f32[320,3840]{1,0:T(8,128)}, f32[320,1280]{1,0:T(8,128)}, f32[320,5120]{1,0:T(8,128)}, f32[1280,1280]{1,0:T(8,128)}), (f32[320,3840]{1,0:T(8,128)}, f32[320,1280]{1,0:T(8,128)}, f32[320,5120]{1,0:T(8,128)}, ...) | async-done | bytes 19660816 | tf_op jit(solution)/shard_map/psum | solution.py:125
  1869.2 5.4 copy.124
  1876.4 3.2 copy.126
  (182 shorter events, 30.9 us)
Async XLA Ops:
  7.2 4.9 copy-start.40
  7.2 5.2 copy-start.41
  7.2 5.4 copy-start.42
  7.2 5.6 copy-start.43
  7.2 5.9 copy-start.44
  7.2 6.1 copy-start.45
  7.3 6.4 copy-start.39
  7.3 20.9 %copy-start.34 = (s32[3,512]{1,0:T(4,128)S(1)}, s32[3,512]{1,0:T(4,128)}, u32[]{:S(2)}) copy-start(s32[3,512]{1,0:T(4,128)} %param.15) | copy-start | bytes 18436
  7.3 21.0 %copy-start.22 = (bf16[33,320]{1,0:T(8,128)(2,1)S(1)}, bf16[33,320]{1,0:T(8,128)(2,1)}, u32[]{:S(2)}) copy-start(bf16[33,320]{1,0:T(8,128)(2,1)} %param.17) | copy-start | bytes 63364
  7.3 72.5 %all-gather.7.cloned.1.call-start = ((), (), s32[]{:S(2)}) async-start(), calls=%async_computation.5 | async-start | bytes 12288000 | tf_op jit(solution)/shard_map/all_gather | solution.py:122
  8.0 217.7 %all-gather.9.cloned.1.call-start = ((), (), s32[]{:S(2)}) async-start(), calls=%async_computation.6 | async-start | bytes 4096000 | tf_op jit(solution)/shard_map/all_gather | solution.py:122
  8.8 33.2 %copy-start.37 = (bf16[1280]{0:T(1024)(128)(2,1)S(1)}, bf16[1280]{0:T(1024)(128)(2,1)}, u32[]{:S(2)}) copy-start(bf16[1280]{0:T(1024)(128)(2,1)} %param.27) | copy-start | bytes 7684
  8.8 230.8 %all-gather.11.cloned.1.call-start = ((), (), s32[]{:S(2)}) async-start(), calls=%async_computation.7 | async-start | bytes 16384000 | tf_op jit(solution)/shard_map/all_gather | solution.py:122
  9.5 351.0 %all-gather.13.cloned.1.call-start = ((), (), s32[]{:S(2)}) async-start(), calls=%async_computation.8 | async-start | bytes 16384000 | tf_op jit(solution)/shard_map/all_gather | solution.py:122
  10.1 782.5 %reduce-scatter.10.cloned.1.call-start = ((), (), s32[]{:S(2)}) async-start(), calls=%async_computation.10 | async-start | bytes 8192000 | tf_op jit(solution)/shard_map/reduce_scatter | solution.py:125
  28.1 75.5 %copy-start.23 = (f32[1280]{0:T(1024)}, f32[1280]{0:T(1024)S(1)}, u32[]{:S(2)}) copy-start(f32[1280]{0:T(1024)S(1)} %convert_element_type.108) | copy-start | bytes 15364
  28.1 75.5 %copy-start.25 = (f32[1280]{0:T(1024)}, f32[1280]{0:T(1024)S(1)}, u32[]{:S(2)}) copy-start(f32[1280]{0:T(1024)S(1)} %convert_element_type.109) | copy-start | bytes 15364
  36.1 67.5 %copy-start.16 = (f32[3,512]{1,0:T(4,128)}, f32[3,512]{1,0:T(4,128)S(1)}, u32[]{:S(2)}) copy-start(f32[3,512]{1,0:T(4,128)S(1)} %broadcast_multiply_fusion.5) | copy-start | bytes 18436
  39.2 64.4 %copy-start.32 = (f32[3,512]{1,0:T(4,128)}, f32[3,512]{1,0:T(4,128)S(1)}, u32[]{:S(2)}) copy-start(f32[3,512]{1,0:T(4,128)S(1)} %add_rsqrt_fusion.1) | copy-start | bytes 18436
  40.2 117.8 %copy-start.8 = (f32[512,32]{0,1:T(8,128)}, f32[512,32]{0,1:T(8,128)S(1)}, u32[]{:S(2)}) copy-start(f32[512,32]{0,1:T(8,128)S(1)} %get-tuple-element.81) | copy-start | bytes 196612
  166.6 30.1 %copy-start.3 = (bf16[3,512,20,32]{1,3,2,0:T(8,128)(2,1)}, bf16[3,512,20,32]{1,3,2,0:T(8,128)(2,1)S(1)}, u32[]{:S(2)}) copy-start(bf16[3,512,20,32]{1,3,2,0:T(8,128)(2,1)S(1)} %get-tuple-element.73) | copy-start | bytes 5898244
  196.7 29.0 %copy-start.11 = (f32[3,20,512]{2,1,0:T(8,128)}, f32[3,20,512]{2,1,0:T(8,128)S(1)}, u32[]{:S(2)}) copy-start(f32[3,20,512]{2,1,0:T(8,128)S(1)} %get-tuple-element.84) | copy-start | bytes 368644
  196.7 29.0 %copy-start.29 = (f32[1280]{0:T(1024)S(1)}, f32[1280]{0:T(1024)}, u32[]{:S(2)}) copy-start(f32[1280]{0:T(1024)} %convert_element_type.116) | copy-start | bytes 15364
  235.4 200.0 %copy-start.14 = (f32[3,512]{1,0:T(4,128)}, f32[3,512]{1,0:T(4,128)S(1)}, u32[]{:S(2)}) copy-start(f32[3,512]{1,0:T(4,128)S(1)} %broadcast_multiply_fusion.4) | copy-start | bytes 18436
  239.5 195.9 %copy-start.20 = (f32[3,512]{1,0:T(4,128)}, f32[3,512]{1,0:T(4,128)S(1)}, u32[]{:S(2)}) copy-start(f32[3,512]{1,0:T(4,128)S(1)} %add_rsqrt_fusion) | copy-start | bytes 18436
  435.5 12.2 copy-start.46
  454.8 6.3 copy-start.12
  555.9 18.8 copy-start.4
  593.8 11.1 copy-start.9
  593.8 11.1 copy-start.10
  604.9 224.6 %reduce-scatter.8.cloned.1.call-start = ((), (), s32[]{:S(2)}) async-start(), calls=%async_computation.9 | async-start | bytes 24576000 | tf_op jit(solution)/shard_map/reduce_scatter | solution.py:125
  659.1 6.2 copy-start.6
  659.1 6.2 copy-start.17
  659.1 6.2 copy-start.24
  659.2 6.2 copy-start.26
  659.2 6.2 copy-start.33
  661.0 4.3 copy-start.1
  687.1 333.9 %reduce-scatter.12.cloned.1.call-start = ((), (), s32[]{:S(2)}) async-start(), calls=%async_computation.11 | async-start | bytes 32768000 | tf_op jit(solution)/shard_map/reduce_scatter | solution.py:125
  718.3 494.2 %reduce-scatter.14.cloned.1.call-start = ((), (), s32[]{:S(2)}) async-start(), calls=%async_computation.12 | async-start | bytes 32768000 | tf_op jit(solution)/shard_map/reduce_scatter | solution.py:125
  746.5 500.7 %all-reduce.24.cloned.1.call-start = ((), (), s32[]{:S(2)}) async-start(), calls=%async_computation.15 | async-start | bytes 172032
  756.9 25.7 %copy-start.31 = (f32[3,512]{1,0:T(4,128)S(1)}, f32[3,512]{1,0:T(4,128)}, u32[]{:S(2)}) copy-start(f32[3,512]{1,0:T(4,128)} %copy-done.30) | copy-start | bytes 18436
  756.9 25.7 %copy-start.35 = (s32[3,512]{1,0:T(4,128)S(1)}, s32[3,512]{1,0:T(4,128)}, u32[]{:S(2)}) copy-start(s32[3,512]{1,0:T(4,128)} %param.15) | copy-start | bytes 18436
  782.5 491.7 %reduce-scatter.16.cloned.1.call-start = ((), (), s32[]{:S(2)}) async-start(), calls=%async_computation.13 | async-start | bytes 819200
  792.6 1076.6 %all-reduce.22.cloned.1.call-start = ((), (), s32[]{:S(2)}) async-start(), calls=%async_computation.14 | async-start | bytes 39321600 | tf_op jit(solution)/shard_map/psum | solution.py:125
  1869.2 5.4 copy-start.7
  1869.2 6.5 slice-start.2
  1869.2 7.2 slice-start.3
  1874.5 5.1 slice-start
  (14 other events, 34.1 us)
Sparse Core Ops, SparseCore 0:
  9.7 70.0 all-gather.6
  81.3 29.2 all-gather.8
  112.2 85.0 all-gather.10
  198.7 85.0 all-gather.12
  605.0 60.8 reduce-scatter.9
  687.2 142.1 reduce-scatter.7
  832.0 188.8 reduce-scatter.11
  1023.6 188.8 reduce-scatter.13
  1216.5 30.7 all-reduce.23
  1250.2 23.9 reduce-scatter.15
  1278.9 590.1 all-reduce.21
where the time goes:
time: 1900 us; the launch traced here: 1890 us
  waiting for transfers between devices  1030 us (54%)
  matrix products  487 us (26%)
  other arithmetic  200 us (11%)
  local copies, waits for them, and re-layouts  85.3 us (4%)
  blocking collectives  67.5 us (4%)
    psum x1, waiting for transfers between devices, local_step(): lax.psum(lax.psum_scatter(full_grad, 'fsdp', scatter_dimension=0, tiled=T...  553 us
    dot_general x19, matrix products, f32_einsum(): return jnp.einsum(form, lhs, rhs, preferred_element_type=jnp.float32)  457 us
    reduce_scatter x4, waiting for transfers between devices, local_step(): lax.psum_scatter(full_grad, 'fsdp', scatter_dimension=0, tiled=True)  420 us
    convert_element_type x1, other arithmetic, layer_step(): act_b16 = hidden_act.astype(jnp.bfloat16)  75.5 us
    convert_element_type x1, other arithmetic, layer_step(): d_scores = d_scores.astype(jnp.bfloat16)  50.2 us
    psum x1, blocking collectives, local_step(): lax.psum(lax.psum_scatter(full_grads[0], 'fsdp', scatter_dimension=1, til...  41.4 us
  transfers between devices with their start and end apart: 11, of which 7 were waited for; matrix products, arithmetic and copies ran while one was open for 27% of the time, Pallas kernels for 0%

commit v1 on v0

v1 whole, which is shorter than its diff:
```python
import jax
import jax.numpy as jnp
from jax import lax
from jax.experimental import pallas as pl
from jax.experimental.pallas import tpu as pltpu
from jax.sharding import PartitionSpec as P

HEAD_DIM = 64
MASK_ID = 32
PAD_ID = 1
MASK_RATIO = 0.15 * 0.8
LN_EPS = 1e-5
ROPE_BASE = 10000.0
NEG = -1e30
BF16 = jnp.bfloat16
F32 = jnp.float32


def dot_f32(lhs, rhs, lhs_dim, rhs_dim):
    return lax.dot_general(lhs, rhs, (((lhs_dim,), (rhs_dim,)), ((), ())), preferred_element_type=F32)


def norm_fwd(x_val, gain, bias):
    centered = x_val - jnp.mean(x_val, axis=-1, keepdims=True)
    inv_std = lax.rsqrt(jnp.mean(centered * centered, axis=-1, keepdims=True) + LN_EPS)
    x_hat = centered * inv_std
    return x_hat * gain.astype(F32) + bias.astype(F32), x_hat, inv_std


def norm_bwd(d_out, x_hat, inv_std, gain):
    d_hat = d_out * gain.astype(F32)
    d_x = inv_std * (d_hat - jnp.mean(d_hat, axis=-1, keepdims=True)
                     - x_hat * jnp.mean(d_hat * x_hat, axis=-1, keepdims=True))
    return d_x, jnp.sum(d_out * x_hat, axis=0), jnp.sum(d_out, axis=0)


def rope_tables(seq_len):
    inv_freq = 1.0 / (ROPE_BASE ** (jnp.arange(0, HEAD_DIM, 2, dtype=F32) / HEAD_DIM))
    angles = jnp.arange(seq_len, dtype=F32)[:, None] * inv_freq[None, :]
    cos_tab, sin_tab = jnp.cos(angles), jnp.sin(angles)
    return (jnp.concatenate([cos_tab] * 4, axis=1),
            jnp.concatenate([-sin_tab, sin_tab, -sin_tab, sin_tab], axis=1))


def partner_lanes(x_val):
    lane = lax.broadcasted_iota(jnp.int32, x_val.shape, 1)
    half = HEAD_DIM // 2
    return jnp.where(lane % HEAD_DIM < half, pltpu.roll(x_val, 128 - half, 1), pltpu.roll(x_val, half, 1))


def attn_fwd_kernel(q_in, k_in, v_in, cos_ref, sin_ref, pad_ref, q_out, k_out, v_out, ctx_out):
    cos_tab, sin_tab = cos_ref[...], sin_ref[...]
    q_val = q_in[0] * HEAD_DIM ** -0.5
    q_val = (q_val * cos_tab + partner_lanes(q_val) * sin_tab).astype(BF16)
    k_val = k_in[0]
    k_val = (k_val * cos_tab + partner_lanes(k_val) * sin_tab).astype(BF16)
    v_val = v_in[0].astype(BF16)
    q_out[0], k_out[0], v_out[0] = q_val, k_val, v_val
    low = lax.broadcasted_iota(jnp.int32, q_val.shape, 1) < HEAD_DIM
    pad = pad_ref[0, :1, :] > 0.0
    parts = []
    for head in range(2):
        q_head = jnp.where(low if head == 0 else jnp.logical_not(low), q_val, jnp.zeros_like(q_val))
        scores = jnp.where(pad, NEG, dot_f32(q_head, k_val, 1, 1))
        weight = jnp.exp(scores - jnp.max(scores, axis=1, keepdims=True))
        prob = weight * (1.0 / jnp.sum(weight, axis=1, keepdims=True))
        parts.append(dot_f32(prob.astype(BF16), v_val, 1, 0))
    ctx_out[0] = jnp.where(low, parts[0], parts[1]).astype(BF16)


def attn_bwd_kernel(q_in, k_in, v_in, d_in, cos_ref, sin_ref, pad_ref, dq_out, bias_out):
    q_val, k_val, v_val, d_ctx = q_in[0], k_in[0], v_in[0], d_in[0]
    cos_tab, sin_tab = cos_ref[...], sin_ref[...]
    low = lax.broadcasted_iota(jnp.int32, q_val.shape, 1) < HEAD_DIM
    pad = pad_ref[0, :, :1] > 0.0
    zero = jnp.zeros_like(k_val)
    dq_parts, dk_parts, dv_parts = [], [], []
    for head in range(2):
        mine = low if head == 0 else jnp.logical_not(low)
        scores = jnp.where(pad, NEG, dot_f32(jnp.where(mine, k_val, zero), q_val, 1, 1))
        weight = jnp.exp(scores - jnp.max(scores, axis=0, keepdims=True))
        prob = weight * (1.0 / jnp.sum(weight, axis=0, keepdims=True))
        d_prob = dot_f32(jnp.where(mine, v_val, zero), d_ctx, 1, 1)
        delta = jnp.sum(prob * d_prob, axis=0, keepdims=True)
        d_scores = (prob * (d_prob - delta)).astype(BF16)
        dv_parts.append(dot_f32(prob.astype(BF16), d_ctx, 1, 0))
        dk_parts.append(dot_f32(d_scores, q_val, 1, 0))
        dq_parts.append(dot_f32(d_scores, k_val, 0, 0))
    d_q = jnp.where(low, dq_parts[0], dq_parts[1])
    d_k = jnp.where(low, dk_parts[0], dk_parts[1])
    d_v = jnp.where(low, dv_parts[0], dv_parts[1])
    d_q = (d_q * cos_tab - partner_lanes(d_q) * sin_tab) * HEAD_DIM ** -0.5
    d_k = d_k * cos_tab - partner_lanes(d_k) * sin_tab
    pair = pl.program_id(1)
    model_dim = dq_out.shape[2] // 3
    for i, grad in enumerate((d_q, d_k, d_v)):
        lanes = pl.ds(pl.multiple_of(pair * 128 + i * model_dim, 128), 128)
        dq_out[0, :, lanes] = grad.astype(BF16)
        bias_out[0, :, lanes] = jnp.sum(grad.reshape(-1, 8, 128), axis=0)


def attention_fwd(qkv_proj, cos_tab, sin_tab, pad_row):
    rows, seq, width = qkv_proj.shape
    dim = width // 3
    pairs = dim // 128
    blk = lambda shift: pl.BlockSpec((1, seq, 128), lambda b, p: (b, 0, p + shift))
    tab = pl.BlockSpec((seq, 128), lambda b, p: (0, 0))
    out = jax.ShapeDtypeStruct((rows, seq, dim), BF16)
    return pl.pallas_call(
        attn_fwd_kernel, grid=(rows, pairs),
        in_specs=[blk(0), blk(pairs), blk(2 * pairs), tab, tab,
                  pl.BlockSpec((1, 8, seq), lambda b, p: (b, 0, 0))],
        out_specs=[blk(0)] * 4, out_shape=[out] * 4,
        cost_estimate=pl.CostEstimate(flops=int(3e10), bytes_accessed=rows * seq * dim * 20,
                                      transcendentals=rows * seq * seq * 2 * pairs),
        name='attn_fwd',
    )(qkv_proj, qkv_proj, qkv_proj, cos_tab, sin_tab, pad_row)


def attention_bwd(q_val, k_val, v_val, d_ctx, cos_tab, sin_tab, pad_col):
    rows, seq, dim = q_val.shape
    pairs = dim // 128
    blk = pl.BlockSpec((1, seq, 128), lambda b, p: (b, 0, p))
    tab = pl.BlockSpec((seq, 128), lambda b, p: (0, 0))
    return pl.pallas_call(
        attn_bwd_kernel, grid=(rows, pairs),
        in_specs=[blk] * 4 + [tab, tab, pl.BlockSpec((1, seq, 128), lambda b, p: (b, 0, 0))],
        out_specs=[pl.BlockSpec((1, seq, 3 * dim), lambda b, p: (b, 0, 0)),
                   pl.BlockSpec((1, 8, 3 * dim), lambda b, p: (b, 0, 0))],
        out_shape=[jax.ShapeDtypeStruct((rows, seq, 3 * dim), BF16),
                   jax.ShapeDtypeStruct((rows, 8, 3 * dim), F32)],
        cost_estimate=pl.CostEstimate(flops=int(6e10), bytes_accessed=rows * seq * dim * 14,
                                      transcendentals=rows * seq * seq * 2 * pairs),
        name='attn_bwd',
    )(q_val, k_val, v_val, d_ctx, cos_tab, sin_tab, pad_col)


def fc1_kernel(x_ref, w_ref, bias_ref, act_ref, slope_ref):
    pre = jnp.dot(x_ref[...], w_ref[...], preferred_element_type=F32) + bias_ref[:1, :]
    cdf = 0.5 * (1.0 + lax.erf(pre * 0.5 ** 0.5))
    act_ref[...] = (pre * cdf).astype(BF16)
    slope_ref[...] = cdf + pre * (jnp.exp(-0.5 * pre * pre) * (0.5 / jnp.pi) ** 0.5)


def fc1_gelu(x_val, w_val, bias, tile_m=512, tile_n=512):
    rows, dim = x_val.shape
    width = w_val.shape[1]
    out = pl.BlockSpec((tile_m, tile_n), lambda j, i: (i, j))
    return pl.pallas_call(
        fc1_kernel, grid=(width // tile_n, rows // tile_m),
        in_specs=[pl.BlockSpec((tile_m, dim), lambda j, i: (i, 0)), pl.BlockSpec((dim, tile_n), lambda j, i: (0, j)),
                  pl.BlockSpec((8, tile_n), lambda j, i: (0, j))],
        out_specs=[out, out],
        out_shape=[jax.ShapeDtypeStruct((rows, width), BF16), jax.ShapeDtypeStruct((rows, width), F32)],
        cost_estimate=pl.CostEstimate(flops=2 * rows * dim * width, bytes_accessed=rows * width * 6,
                                      transcendentals=rows * width * 2),
        name='fc1_gelu',
    )(x_val, w_val, bias)


def swap(x_val, axis, size, mask):
    return lax.ppermute(x_val, axis, [(i, i ^ mask) for i in range(size)])


def part(x_val, index, count, dim=0):
    size = x_val.shape[dim] // count
    return lax.dynamic_slice_in_dim(x_val, index * size, size, dim)


class Place:
    def __init__(self):
        fsdp, dp = lax.axis_index('fsdp'), lax.axis_index('dp')
        self.core, self.x = fsdp % 2, fsdp // 2
        self.y, self.z = dp % 2, dp // 2
        self.z0, self.z1 = self.z % 2, self.z // 2


def sum_over_dp(place, kept, arrived):
    total, got = kept, arrived
    for bit, mask in ((place.y, 1), (place.z0, 2), (place.z1, 4)):
        total = total + got
        away = part(total, 1 - bit, 2)
        total = part(total, bit, 2)
        got = swap(away, 'dp', 8, mask)
    total = total + got
    pieces = [total] + [swap(total, 'dp', 8, 2 * step) for step in (1, 2, 3)]
    half = jnp.concatenate([lax.select_n(place.z ^ z_of, *pieces) for z_of in (0, 2, 1, 3)], axis=0)
    other = swap(half, 'dp', 8, 1)
    low = place.y == 0
    return jnp.concatenate([jnp.where(low, half, other), jnp.where(low, other, half)], axis=0)


def quarter_cols(x_val, x_index, core_index, count=1, chunk=0):
    return part(x_val, (2 * x_index + core_index) * count + chunk, 4 * count, 1)


def send_half(place, lhs, rhs, count=1, chunk=0):
    cols = jnp.concatenate([quarter_cols(lhs, i, 1 - place.core, count, chunk) for i in range(2)], axis=1)
    return swap(dot_f32(cols, rhs, 0, 0), 'fsdp', 4, 1)


def own_half(place, got, lhs, rhs, count=1, chunk=0):
    away = dot_f32(quarter_cols(lhs, 1 - place.x, place.core, count, chunk), rhs, 0, 0) + part(got, 1 - place.x, 2)
    arrived = swap(away, 'fsdp', 4, 2)
    kept = dot_f32(quarter_cols(lhs, place.x, place.core, count, chunk), rhs, 0, 0) + part(got, place.x, 2)
    return kept, arrived


def small_sum(place, grads):
    wide = grads.reshape(2, 2, -1, 128)
    mine = lax.dynamic_index_in_dim(wide, place.core, 1, False)
    mine = mine + swap(lax.dynamic_index_in_dim(wide, 1 - place.core, 1, False), 'fsdp', 4, 1)
    own = lax.dynamic_index_in_dim(mine, place.x, 0, False)
    own = own + swap(lax.dynamic_index_in_dim(mine, 1 - place.x, 0, False), 'fsdp', 4, 2)
    for mask in (1, 2, 4):
        own = own + swap(own, 'dp', 8, mask)
    return own.reshape(-1)


def solution(mesh):
    row_spec = P(('dp', 'fsdp'), None)
    act_spec = P(('dp', 'fsdp'), None, None)
    param_specs = (P(None, 'fsdp'),) + (P('fsdp'),) * 12

    def local_step(tokens, grad_y, *shards):
        (embedding, ln1_gain, ln1_bias, w_qkv, b_qkv, w_out, b_out,
         ln2_gain, ln2_bias, w_fc1, b_fc1, w_fc2, b_fc2) = shards
        place = Place()
        batch, seq = tokens.shape
        dim = grad_y.shape[2]
        vocab = embedding.shape[0]
        rows = batch * seq

        small = [embedding, ln1_gain, ln1_bias, b_out, ln2_gain, ln2_bias, b_fc2, b_qkv, b_fc1]
        whole = [lax.all_gather(shard, 'fsdp', axis=shard.ndim - 1, tiled=True) for shard in small]
        embedding, ln1_gain, ln1_bias, b_out, ln2_gain, ln2_bias, b_fc2, b_qkv, b_fc1 = whole
        w_qkv, w_out, w_fc1, w_fc2 = [lax.all_gather(w, 'fsdp', axis=0, tiled=True)
                                      for w in (w_qkv, w_out, w_fc1, w_fc2)]

        one_hot = tokens[:, :, None] == jnp.arange(vocab)[None, None, :]
        is_mask = tokens == MASK_ID
        is_pad = tokens == PAD_ID
        mask_count = jnp.sum(is_mask, axis=1).astype(F32)
        real_count = jnp.sum(jnp.logical_not(is_pad), axis=1).astype(F32)
        factor = (1.0 - MASK_RATIO) / (1.0 - mask_count / real_count)
        keep_scale = jnp.where(is_mask | is_pad, 0.0, factor[:, None]).reshape(rows, 1)
        one_hot = one_hot.reshape(rows, vocab)
        looked_up = dot_f32(one_hot.astype(BF16), embedding, 1, 0)
        x_res = (looked_up * keep_scale).astype(BF16).astype(F32)
        norm_one, hat_one, inv_one = norm_fwd(x_res, ln1_gain, ln1_bias)
        h_one = norm_one.astype(BF16)
        qkv_proj = dot_f32(h_one, w_qkv, 1, 0) + b_qkv.astype(F32)
        cos_tab, sin_tab = rope_tables(seq)
        pad_f32 = is_pad.astype(F32)
        queries, key_rows, values, context = attention_fwd(
            qkv_proj.reshape(batch, seq, 3 * dim), cos_tab, sin_tab, jnp.broadcast_to(pad_f32[:, None, :], (batch, 8, seq)))
        context = context.reshape(rows, dim)
        x_mid = x_res + dot_f32(context, w_out, 1, 0) + b_out.astype(F32)
        norm_two, hat_two, inv_two = norm_fwd(x_mid, ln2_gain, ln2_bias)
        h_two = norm_two.astype(BF16)
        act_b16, slope = fc1_gelu(h_two, w_fc1, jnp.broadcast_to(b_fc1.astype(F32)[None, :], (8, b_fc1.size)))

        grad_y = grad_y.reshape(rows, dim)
        grad_res = grad_y.astype(F32)
        got_fc2 = [send_half(place, act_b16, grad_y, 2, j) for j in range(2)]
        d_pre = dot_f32(grad_y, w_fc2, 1, 1) * slope
        g_b_fc1 = jnp.sum(d_pre, axis=0)
        d_pre = d_pre.astype(BF16)
        sums_fc2 = [own_half(place, got_fc2[j], act_b16, grad_y, 2, j) for j in range(2)]
        pre_cols = [d_pre[:, :2 * dim], d_pre[:, 2 * dim:]]
        got_fc1 = [send_half(place, h_two, pre_cols[j]) for j in range(2)]
        d_two, g_ln2_gain, g_ln2_bias = norm_bwd(dot_f32(d_pre, w_fc1, 1, 1), hat_two, inv_two, ln2_gain)
        sums_fc1 = [own_half(place, got_fc1[j], h_two, pre_cols[j]) for j in range(2)]
        d_mid = grad_res + d_two
        g_b_out = jnp.sum(d_mid, axis=0)
        g_b_fc2 = jnp.sum(grad_res, axis=0)
        d_mid_b16 = d_mid.astype(BF16)
        d_ctx = dot_f32(d_mid_b16, w_out, 1, 1).astype(BF16)
        got_out = send_half(place, context, d_mid_b16)
        d_qkv, g_b_qkv = attention_bwd(queries, key_rows, values, d_ctx.reshape(batch, seq, dim),
                                       cos_tab, sin_tab, jnp.broadcast_to(pad_f32[:, :, None], (batch, seq, 128)))
        sums_out = own_half(place, got_out, context, d_mid_b16)
        d_qkv = d_qkv.reshape(rows, 3 * dim)
        g_b_qkv = jnp.sum(g_b_qkv, axis=(0, 1))
        half_qkv = 3 * dim // 2
        qkv_cols = [d_qkv[:, :half_qkv], d_qkv[:, half_qkv:]]
        got_qkv = [send_half(place, h_one, qkv_cols[j]) for j in range(2)]
        d_one, g_ln1_gain, g_ln1_bias = norm_bwd(dot_f32(d_qkv, w_qkv, 1, 1), hat_one, inv_one, ln1_gain)
        sums_qkv = [own_half(place, got_qkv[j], h_one, qkv_cols[j]) for j in range(2)]
        d_in = d_mid + d_one
        g_embedding = dot_f32(one_hot.astype(F32), d_in * keep_scale, 0, 0)
        hidden = (x_mid + dot_f32(act_b16, w_fc2, 1, 0) + b_fc2.astype(F32)).astype(BF16)

        g_w_fc2 = jnp.concatenate([sum_over_dp(place, *sums_fc2[j]) for j in range(2)], axis=0)
        g_w_fc1 = jnp.concatenate([sum_over_dp(place, *sums_fc1[j]) for j in range(2)], axis=1)
        g_w_out = sum_over_dp(place, *sums_out)
        g_w_qkv = jnp.concatenate([sum_over_dp(place, *sums_qkv[j]) for j in range(2)], axis=1)

        small_grads = [g_embedding.reshape(vocab, 4, -1).transpose(1, 0, 2).reshape(4, -1)]
        small_grads += [g.reshape(4, -1) for g in (g_ln1_gain, g_ln1_bias, g_b_out, g_ln2_gain, g_ln2_bias,
                                                   g_b_fc2, g_b_qkv, g_b_fc1)]
        summed = small_sum(place, jnp.concatenate(small_grads, axis=1))
        outs, at = [], 0
        for i, grad in enumerate(small_grads):
            piece = summed[at:at + grad.shape[1]]
            at += grad.shape[1]
            outs.append(piece.reshape(vocab, -1) if i == 0 else piece)
        (g_embedding, g_ln1_gain, g_ln1_bias, g_b_out, g_ln2_gain, g_ln2_bias, g_b_fc2, g_b_qkv, g_b_fc1) = outs
        return (hidden.reshape(batch, seq, dim), g_embedding, g_ln1_gain, g_ln1_bias, g_w_qkv, g_b_qkv, g_w_out,
                g_b_out, g_ln2_gain, g_ln2_bias, g_w_fc1, g_b_fc1, g_w_fc2, g_b_fc2)

    return jax.shard_map(local_step, mesh=mesh, in_specs=(row_spec, act_spec) + param_specs,
                         out_specs=(act_spec,) + param_specs, check_vma=False)
```

time: 1900 us -> 1560 us (0.82)
  waiting for transfers between devices: 1030 us -> 743 us
  matrix products: 487 us -> 299 us
  Pallas kernels: 0 us -> 176 us
  starting transfers between devices: 0.44 us -> 122 us
  other arithmetic: 200 us -> 81.5 us
  blocking collectives: 67.5 us -> 25.3 us
    ppermute x0 -> x68, waiting for transfers between devices: none -> 660 us  [swap(): return lax.ppermute(x_val, axis, [(i, i ^ mask) for i in range(size)])]
    psum x1 -> x0, waiting for transfers between devices: 553 us -> none  [local_step(): lax.psum(lax.psum_scatter(full_grad, 'fsdp', scatter_dimension=0, tiled=T...]
    reduce_scatter x4 -> x0, waiting for transfers between devices: 420 us -> none  [local_step(): lax.psum_scatter(full_grad, 'fsdp', scatter_dimension=0, tiled=True)]
    pallas_call x0 -> x3, Pallas kernels: none -> 176 us  [the longest x1 75.3 us: attention_bwd(): pl.pallas_call(attn_bwd_kernel, grid=(rows, pairs), in_specs=[blk] * 4 +...]
    dot_general x19 -> x30, matrix products: 457 us -> 299 us  [dot_f32(): lax.dot_general(lhs, rhs, (((lhs_dim,), (rhs_dim,)), ((), ())), preferred...]
    convert_element_type x11 -> x12, other arithmetic: 137 us -> 4.46 us  [the longest x1 1.92 us: local_step(): h_one = norm_one.astype(BF16)]
    ppermute x0 -> x68, starting transfers between devices: none -> 122 us  [swap(): return lax.ppermute(x_val, axis, [(i, i ^ mask) for i in range(size)])]
    all_gather x4, waiting for transfers between devices: 31.5 us -> 80.6 us  [local_step(): lax.all_gather(w, 'fsdp', axis=0, tiled=True)]
  transfers between devices with their start and end apart: 11 -> 72, of which waited for: 7 -> 36; matrix products, arithmetic and copies ran while one was open for 27% -> 18% of each run, Pallas kernels for 0% -> 7%
where the time goes in v1:
time: 1560 us; the launch traced here: 1540 us
  waiting for transfers between devices  743 us (48%)
  matrix products  299 us (19%)
  Pallas kernels  176 us (11%)
  starting transfers between devices  122 us (8%)
  other arithmetic  81.5 us (5%)
  local copies, waits for them, and re-layouts  72.2 us (5%)
  blocking collectives  25.3 us (2%)
  between operations  17.2 us (1%)
    ppermute x68, waiting for transfers between devices, swap(): return lax.ppermute(x_val, axis, [(i, i ^ mask) for i in range(size)])  660 us
    dot_general x30, matrix products, dot_f32(): lax.dot_general(lhs, rhs, (((lhs_dim,), (rhs_dim,)), ((), ())), preferred...  299 us
    ppermute x68, starting transfers between devices, swap(): return lax.ppermute(x_val, axis, [(i, i ^ mask) for i in range(size)])  122 us
    all_gather x4, waiting for transfers between devices, local_step(): lax.all_gather(w, 'fsdp', axis=0, tiled=True)  80.6 us
    pallas_call x1, Pallas kernels, attention_bwd(): pl.pallas_call(attn_bwd_kernel, grid=(rows, pairs), in_specs=[blk] * 4 +...  75.3 us
    pallas_call x1, Pallas kernels, fc1_gelu(): pl.pallas_call(fc1_kernel, grid=(width // tile_n, rows // tile_m), in_spe...  52.9 us
    pallas_call x1, Pallas kernels, attention_fwd(): pl.pallas_call(attn_fwd_kernel, grid=(rows, pairs), in_specs=[blk(0), blk...  48.2 us
  transfers between devices with their start and end apart: 72, of which 36 were waited for; matrix products, arithmetic and copies ran while one was open for 18% of the time, Pallas kernels for 7%

profile of v1, /device:TPU:0, one launch (start us, length us, event | category | flops | bytes accessed | tf_op | source)
XLA Modules:
  0.0 1536.1 jit_solution(16381782912789453207)
XLA Ops:
  14.0 13.7 all-reduce.7
  55.4 24.2 %all-gather.7.cloned.1.call-done = bf16[1280,3840]{1,0:T(8,128)(2,1)} async-done(((bf16[320,3840]{1,0:T(8,128)(2,1)}), bf16[1280,3840]{1,0:T(8,128)(2,1)}) %all-gather.7.cloned.1.call-update) | async-done | bytes 9830416 | tf_op jit(solution)/shard_map/all_gather | solution.py:237
  79.7 22.1 %convolution_add_fusion = f32[1536,3840]{1,0:T(8,128)} fusion(bf16[1536,1280]{1,0:T(8,128)(2,1)} %copy-done.14, bf16[1280,3840]{1,0:T(8,128)(2,1)} %all-gather.7.cloned.1.call-done, f32[3840]{0:T(1024)S(1)} %convert_element_type.90), kind=kOutput, calls=%fused_computation.1 | convolution fusion | flops 15105392640 | bytes 37370880 | tf_op jit(solution)/shard_map/dot_general | solution.py:20
  102.4 48.2 %attn_fwd.1 = (bf16[3,512,1280]{2,1,0:T(8,128)(2,1)}, bf16[3,512,1280]{2,1,0:T(8,128)(2,1)}, bf16[3,512,1280]{2,1,0:T(8,128)(2,1)}, bf16[3,512,1280]{2,1,0:T(8,128)(2,1)}) custom-call(f32[3,512,3840]{2,1,0:T(8,128)} %bitcast.80, f32[3,512,3840]{2,1,0:T(8,128)} %bitcast.81, f32[3,512,3840]{2,1,0:T(8,128)} %bitcast.82, f32[512,128]{1,0:T(8,128)} %get-tuple-element.122.cos_ref, ...), custom_call_target="tpu_custom_call" | custom-call | flops 30000001024 | bytes 39321600 | tf_op jit(solution)/shard_map/attn_fwd/pallas_call | solution.py:109
  150.7 9.3 fusion.130
  173.8 23.4 %all-gather.11.cloned.1.call-done.w_ref = bf16[1280,5120]{1,0:T(8,128)(2,1)} async-done(((bf16[320,5120]{1,0:T(8,128)(2,1)}), bf16[1280,5120]{1,0:T(8,128)(2,1)}) %all-gather.11.cloned.1.call-update) | async-done | bytes 13107216 | tf_op jit(solution)/shard_map/all_gather | solution.py:237
  197.9 52.9 %fc1_gelu.1 = (bf16[1536,5120]{1,0:T(8,128)(2,1)}, f32[1536,5120]{1,0:T(8,128)}) custom-call(bf16[1536,1280]{1,0:T(8,128)(2,1)} %copy-done.11, bf16[1280,5120]{1,0:T(8,128)(2,1)} %all-gather.11.cloned.1.call-done.w_ref, f32[8,5120]{1,0:T(8,128)} %broadcast_in_dim.21.bias_ref), custom_call_target="tpu_custom_call" | custom-call | flops 20132659200 | bytes 47185920 | tf_op jit(solution)/shard_map/fc1_gelu/pallas_call | solution.py:149
  250.7 33.0 %all-gather.13.cloned.1.call-done = bf16[5120,1280]{1,0:T(8,128)(2,1)} async-done(((bf16[1280,1280]{1,0:T(8,128)(2,1)}), bf16[5120,1280]{1,0:T(8,128)(2,1)}) %all-gather.13.cloned.1.call-update) | async-done | bytes 13107216 | tf_op jit(solution)/shard_map/all_gather | solution.py:237
  283.7 29.6 %fusion.128 = (f32[5120]{0:T(1024)}, bf16[1536,5120]{1,0:T(8,128)(2,1)}) fusion(f32[1536,5120]{1,0:T(8,128)} %get-tuple-element.24, bf16[1536,1280]{1,0:T(8,128)(2,1)} %bitcast.60, bf16[5120,1280]{1,0:T(8,128)(2,1)} %all-gather.13.cloned.1.call-done), kind=kOutput, calls=%fused_computation.269 | convolution fusion | flops 20156248064 | bytes 64245760 | tf_op jit(solution)/shard_map/dot_general | solution.py:20
  313.3 30.0 %fusion.132 = (f32[1280]{0:T(1024)}, f32[1536,1280]{0,1:T(8,128)}) fusion(bf16[1536,5120]{1,0:T(8,128)(2,1)} %get-tuple-element.50, bf16[1280,5120]{1,0:T(8,128)(2,1)} %all-gather.11.cloned.1.call-done.w_ref), kind=kOutput, calls=%fused_computation.273 | convolution fusion | flops 20134623232 | bytes 36705280 | tf_op jit(solution)/shard_map/dot_general | solution.py:20
  343.3 9.2 copy.47
  379.3 75.3 %attn_bwd.1 = (bf16[3,512,3840]{2,1,0:T(8,128)(2,1)}, f32[3,8,3840]{2,1,0:T(8,128)}) custom-call(bf16[3,512,1280]{2,1,0:T(8,128)(2,1)} %get-tuple-element.25.q_in, bf16[3,512,1280]{2,1,0:T(8,128)(2,1)} %get-tuple-element.26.k_in, bf16[3,512,1280]{2,1,0:T(8,128)(2,1)} %get-tuple-element.27.v_in, bf16[3,512,1280]{2,1,0:T(8,128)(2,1)} %bitcast.91, ...), custom_call_target="tpu_custom_call" | custom-call | flops 60000002048 | bytes 27525120 | tf_op jit(solution)/shard_map/attn_bwd/pallas_call | solution.py:125
  454.6 9.5 fusion.34
  470.4 17.8 %fusion.131 = (f32[1280]{0:T(1024)S(1)}, f32[1536,1280]{0,1:T(8,128)}) fusion(bf16[1536,3840]{1,0:T(8,128)(2,1)S(1)} %bitcast.89, bf16[1280,3840]{1,0:T(8,128)(2,1)S(1)} %bitcast.79), kind=kOutput, calls=%fused_computation.272 | convolution fusion | flops 15101459456 | bytes 29496320 | tf_op jit(solution)/shard_map/dot_general | solution.py:20
  488.2 9.2 copy.48
  539.7 26.5 %fusion.19 = bf16[1536,1280]{1,0:T(8,128)(2,1)} fusion(f32[1536,1280]{1,0:T(8,128)} %copy-done, bf16[1536,5120]{1,0:T(8,128)(2,1)S(1)} %bitcast.69, bf16[5120,1280]{1,0:T(8,128)(2,1)} %all-gather.13.cloned.1.call-done, f32[1280]{0:T(1024)S(1)} %copy-done.51), kind=kOutput, calls=%fused_computation.32 | convolution fusion | flops 20138557440 | bytes 40637440 | tf_op jit(solution)/shard_map/dot_general | solution.py:20
  566.2 10.4 fusion.48
  576.6 10.0 fusion.22
  586.6 10.5 fusion.28
  622.3 19.0 %collective-permute-done.24 = f32[320,1280]{1,0:T(8,128)} collective-permute-done((f32[320,1280]{1,0:T(8,128)}, f32[320,1280]{1,0:T(8,128)}, u32[]{:S(2)}, u32[]{:S(2)}) %collective-permute-start.24) | collective-permute-done | bytes 1638432 | tf_op jit(solution)/shard_map/ppermute | solution.py:162
  649.9 13.2 collective-permute-done.2
  715.5 12.2 collective-permute-done.29
  747.7 8.7 dynamic-slice_add_fusion.2
  764.9 8.7 dynamic-slice_add_fusion.3
  781.8 20.0 %collective-permute-done.15 = f32[320,1920]{1,0:T(8,128)S(1)} collective-permute-done((f32[320,1920]{1,0:T(8,128)}, f32[320,1920]{1,0:T(8,128)S(1)}, u32[]{:S(2)}, u32[]{:S(2)}) %collective-permute-start.15) | collective-permute-done | bytes 2457632 | tf_op jit(solution)/shard_map/ppermute | solution.py:162
  805.9 48.6 %collective-permute-done.6 = f32[320,1920]{1,0:T(8,128)S(1)} collective-permute-done((f32[320,1920]{1,0:T(8,128)}, f32[320,1920]{1,0:T(8,128)S(1)}, u32[]{:S(2)}, u32[]{:S(2)}) %collective-permute-start.6) | collective-permute-done | bytes 2457632 | tf_op jit(solution)/shard_map/ppermute | solution.py:162
  862.3 19.1 %collective-permute-done.7 = f32[160,1920]{1,0:T(8,128)S(1)} collective-permute-done((f32[160,1920]{1,0:T(8,128)S(1)}, f32[160,1920]{1,0:T(8,128)S(1)}, u32[]{:S(2)}, u32[]{:S(2)}) %collective-permute-start.7) | collective-permute-done | bytes 1228832 | tf_op jit(solution)/shard_map/ppermute | solution.py:162
  884.7 15.8 %collective-permute-done.8 = f32[80,1920]{1,0:T(8,128)S(1)} collective-permute-done((f32[80,1920]{1,0:T(8,128)S(1)}, f32[80,1920]{1,0:T(8,128)S(1)}, u32[]{:S(2)}, u32[]{:S(2)}) %collective-permute-start.8) | collective-permute-done | bytes 614432 | tf_op jit(solution)/shard_map/ppermute | solution.py:162
  905.4 22.5 %collective-permute-done.9 = f32[40,1920]{1,0:T(8,128)S(1)} collective-permute-done((f32[40,1920]{1,0:T(8,128)S(1)}, f32[40,1920]{1,0:T(8,128)S(1)}, u32[]{:S(2)}, u32[]{:S(2)}) %collective-permute-start.9) | collective-permute-done | bytes 307232 | tf_op jit(solution)/shard_map/ppermute | solution.py:162
  941.0 15.6 %collective-permute-start.10 = (f32[40,1920]{1,0:T(8,128)S(1)}, f32[40,1920]{1,0:T(8,128)S(1)}, u32[]{:S(2)}, u32[]{:S(2)}) collective-permute-start(f32[40,1920]{1,0:T(8,128)S(1)} %dynamic-slice_add_fusion.26), channel_id=1, source_target_pairs={{0,8},{4,12},{8,0},{12,4},{16,24},{20,28},{24,16},{28,20},{1,9},{5... | collective-permute-start | bytes 921608 | tf_op jit(solution)/shard_map/ppermute | solution.py:162
  975.0 20.0 %collective-permute-done.33 = f32[320,2560]{1,0:T(8,128)S(1)} collective-permute-done((f32[320,2560]{1,0:T(8,128)}, f32[320,2560]{1,0:T(8,128)S(1)}, u32[]{:S(2)}, u32[]{:S(2)}) %collective-permute-start.33) | collective-permute-done | bytes 3276832 | tf_op jit(solution)/shard_map/ppermute | solution.py:162
  1000.8 64.3 %collective-permute-done.60 = f32[640,1280]{1,0:T(8,128)S(1)} collective-permute-done((f32[640,1280]{1,0:T(8,128)S(1)}, f32[640,1280]{1,0:T(8,128)S(1)}, u32[]{:S(2)}, u32[]{:S(2)}) %collective-permute-start.60) | collective-permute-done | bytes 3276832 | tf_op jit(solution)/shard_map/ppermute | solution.py:162
  1070.6 62.5 %collective-permute-done.51 = f32[640,1280]{1,0:T(8,128)S(1)} collective-permute-done((f32[640,1280]{1,0:T(8,128)}, f32[640,1280]{1,0:T(8,128)S(1)}, u32[]{:S(2)}, u32[]{:S(2)}) %collective-permute-start.51) | collective-permute-done | bytes 3276832 | tf_op jit(solution)/shard_map/ppermute | solution.py:162
  1146.1 25.9 %collective-permute-done.61 = f32[320,1280]{1,0:T(8,128)S(1)} collective-permute-done((f32[320,1280]{1,0:T(8,128)}, f32[320,1280]{1,0:T(8,128)S(1)}, u32[]{:S(2)}, u32[]{:S(2)}) %collective-permute-start.61) | collective-permute-done | bytes 1638432 | tf_op jit(solution)/shard_map/ppermute | solution.py:162
  1174.0 30.0 %collective-permute-done.52 = f32[320,1280]{1,0:T(8,128)} collective-permute-done((f32[320,1280]{1,0:T(8,128)}, f32[320,1280]{1,0:T(8,128)}, u32[]{:S(2)}, u32[]{:S(2)}) %collective-permute-start.52) | collective-permute-done | bytes 1638432 | tf_op jit(solution)/shard_map/ppermute | solution.py:162
  1212.3 28.2 %collective-permute-done.53 = f32[160,1280]{1,0:T(8,128)S(1)} collective-permute-done((f32[160,1280]{1,0:T(8,128)S(1)}, f32[160,1280]{1,0:T(8,128)S(1)}, u32[]{:S(2)}, u32[]{:S(2)}) %collective-permute-start.53) | collective-permute-done | bytes 819232 | tf_op jit(solution)/shard_map/ppermute | solution.py:162
  1245.9 37.1 %collective-permute-done.36 = f32[40,2560]{1,0:T(8,128)S(1)} collective-permute-done((f32[40,2560]{1,0:T(8,128)S(1)}, f32[40,2560]{1,0:T(8,128)S(1)}, u32[]{:S(2)}, u32[]{:S(2)}) %collective-permute-start.36) | collective-permute-done | bytes 409632 | tf_op jit(solution)/shard_map/ppermute | solution.py:162
  1283.1 13.1 collective-permute-done.63
  1296.3 17.5 %collective-permute-done.54 = f32[80,1280]{1,0:T(8,128)S(1)} collective-permute-done((f32[80,1280]{1,0:T(8,128)S(1)}, f32[80,1280]{1,0:T(8,128)S(1)}, u32[]{:S(2)}, u32[]{:S(2)}) %collective-permute-start.54) | collective-permute-done | bytes 409632 | tf_op jit(solution)/shard_map/ppermute | solution.py:162
  1315.8 11.2 collective-permute-done.47
  1327.0 18.6 %collective-permute-start.65 = (f32[80,1280]{1,0:T(8,128)S(1)}, f32[80,1280]{1,0:T(8,128)S(1)}, u32[]{:S(2)}, u32[]{:S(2)}) collective-permute-start(f32[80,1280]{1,0:T(8,128)S(1)} %dynamic-slice_add_fusion.20), channel_id=1, source_target_pairs={{0,16},{4,20},{8,24},{12,28},{16,0},{20,4},{24,8},{28,12},{1,17},{... | collective-permute-start | bytes 1228808 | tf_op jit(solution)/shard_map/ppermute | solution.py:162
  1347.7 14.4 collective-permute-done.38
  1362.1 18.6 %collective-permute-start.56 = (f32[80,1280]{1,0:T(8,128)S(1)}, f32[80,1280]{1,0:T(8,128)S(1)}, u32[]{:S(2)}, u32[]{:S(2)}) collective-permute-start(f32[80,1280]{1,0:T(8,128)S(1)} %dynamic-slice_add_fusion.21), channel_id=1, source_target_pairs={{0,16},{4,20},{8,24},{12,28},{16,0},{20,4},{24,8},{28,12},{1,17},{... | collective-permute-start | bytes 1228808 | tf_op jit(solution)/shard_map/ppermute | solution.py:162
  1383.0 14.2 collective-permute-done.65
  1399.5 15.2 collective-permute-done.56
  1417.2 18.7 %collective-permute-done.49 = f32[160,2560]{1,0:T(8,128)S(1)} collective-permute-done((f32[160,2560]{1,0:T(8,128)S(1)}, f32[160,2560]{1,0:T(8,128)S(1)}, u32[]{:S(2)}, u32[]{:S(2)}) %collective-permute-start.49) | collective-permute-done | bytes 1638432 | tf_op jit(solution)/shard_map/ppermute | solution.py:162
  1436.1 69.9 %collective-permute-done.67 = f32[320,1280]{1,0:T(8,128)S(1)} collective-permute-done((f32[320,1280]{1,0:T(8,128)S(1)}, f32[320,1280]{1,0:T(8,128)S(1)}, u32[]{:S(2)}, u32[]{:S(2)}) %collective-permute-start.67) | collective-permute-done | bytes 1638432 | tf_op jit(solution)/shard_map/ppermute | solution.py:162
  1510.0 14.4 collective-permute-done.58
  (439 shorter events, 357.0 us)
Async XLA Ops:
  7.2 72.5 %all-gather.7.cloned.1.call-start = ((), (), s32[]{:S(2)}) async-start(), calls=%async_computation | async-start | bytes 12288000 | tf_op jit(solution)/shard_map/all_gather | solution.py:237
  7.9 142.8 %all-gather.9.cloned.1.call-start = ((), (), s32[]{:S(2)}) async-start(), calls=%async_computation.1 | async-start | bytes 4096000 | tf_op jit(solution)/shard_map/all_gather | solution.py:237
  8.8 188.4 %all-gather.11.cloned.1.call-start = ((), (), s32[]{:S(2)}) async-start(), calls=%async_computation.2 | async-start | bytes 16384000 | tf_op jit(solution)/shard_map/all_gather | solution.py:237
  9.5 274.2 %all-gather.13.cloned.1.call-start = ((), (), s32[]{:S(2)}) async-start(), calls=%async_computation.3 | async-start | bytes 16384000 | tf_op jit(solution)/shard_map/all_gather | solution.py:237
  524.6 95.1 %collective-permute-start = (f32[2,115,128]{2,1,0:T(8,128)}, f32[2,115,128]{2,1,0:T(8,128)}, u32[]{:S(2)}, u32[]{:S(2)}) collective-permute-start(f32[2,115,128]{2,1,0:T(8,128)} %dynamic-slice_bitcast_fusion), channel_id=1, source_target_pairs={{0,1},{1,0},{2,3},{3,2},{4,5},{5,4},{6,7},{7,6},{8,9},{9,8},{10,11... | collective-permute-start | bytes 353288 | tf_op jit(solution)/shard_map/ppermute | solution.py:162
  524.9 158.9 %collective-permute-start.14 = (f32[640,1920]{1,0:T(8,128)}, f32[640,1920]{1,0:T(8,128)}, u32[]{:S(2)}, u32[]{:S(2)}) collective-permute-start(f32[640,1920]{1,0:T(8,128)} %fusion.34), channel_id=1, source_target_pairs={{0,1},{1,0},{2,3},{3,2},{4,5},{5,4},{6,7},{7,6},{8,9},{9,8},{10,11... | collective-permute-start | bytes 14745608 | tf_op jit(solution)/shard_map/ppermute | solution.py:162
  525.1 189.7 %collective-permute-start.5 = (f32[640,1920]{1,0:T(8,128)}, f32[640,1920]{1,0:T(8,128)}, u32[]{:S(2)}, u32[]{:S(2)}) collective-permute-start(f32[640,1920]{1,0:T(8,128)} %fusion.40), channel_id=1, source_target_pairs={{0,1},{1,0},{2,3},{3,2},{4,5},{5,4},{6,7},{7,6},{8,9},{9,8},{10,11... | collective-permute-start | bytes 14745608 | tf_op jit(solution)/shard_map/ppermute | solution.py:162
  532.5 64.6 %collective-permute-start.23 = (f32[640,1280]{1,0:T(8,128)}, f32[640,1280]{1,0:T(8,128)S(1)}, u32[]{:S(2)}, u32[]{:S(2)}) collective-permute-start(f32[640,1280]{1,0:T(8,128)} %fusion.52), channel_id=1, source_target_pairs={{0,1},{1,0},{2,3},{3,2},{4,5},{5,4},{6,7},{7,6},{8,9},{9,8},{10,11... | collective-permute-start | bytes 9830408 | tf_op jit(solution)/shard_map/ppermute | solution.py:162
  602.7 38.7 %collective-permute-start.24 = (f32[320,1280]{1,0:T(8,128)}, f32[320,1280]{1,0:T(8,128)}, u32[]{:S(2)}, u32[]{:S(2)}) collective-permute-start(f32[320,1280]{1,0:T(8,128)} %dynamic-slice_add_fusion.10), channel_id=1, source_target_pairs={{0,2},{1,3},{2,0},{3,1},{4,6},{5,7},{6,4},{7,5},{8,10},{9,11},{10,... | collective-permute-start | bytes 4915208 | tf_op jit(solution)/shard_map/ppermute | solution.py:162
  619.6 126.9 %collective-permute-start.41 = (f32[640,2560]{1,0:T(8,128)}, f32[640,2560]{1,0:T(8,128)}, u32[]{:S(2)}, u32[]{:S(2)}) collective-permute-start(f32[640,2560]{1,0:T(8,128)} %fusion.22), channel_id=1, source_target_pairs={{0,1},{1,0},{2,3},{3,2},{4,5},{5,4},{6,7},{7,6},{8,9},{9,8},{10,11... | collective-permute-start | bytes 19660808 | tf_op jit(solution)/shard_map/ppermute | solution.py:162
  663.2 93.3 %collective-permute-start.59 = (f32[1280,1280]{1,0:T(8,128)}, f32[1280,1280]{1,0:T(8,128)}, u32[]{:S(2)}, u32[]{:S(2)}) collective-permute-start(f32[1280,1280]{1,0:T(8,128)} %fusion.48), channel_id=1, source_target_pairs={{0,1},{1,0},{2,3},{3,2},{4,5},{5,4},{6,7},{7,6},{8,9},{9,8},{10,11... | collective-permute-start | bytes 19660808 | tf_op jit(solution)/shard_map/ppermute | solution.py:162
  683.8 80.1 %collective-permute-start.32 = (f32[640,2560]{1,0:T(8,128)}, f32[640,2560]{1,0:T(8,128)}, u32[]{:S(2)}, u32[]{:S(2)}) collective-permute-start(f32[640,2560]{1,0:T(8,128)} %fusion.28), channel_id=1, source_target_pairs={{0,1},{1,0},{2,3},{3,2},{4,5},{5,4},{6,7},{7,6},{8,9},{9,8},{10,11... | collective-permute-start | bytes 19660808 | tf_op jit(solution)/shard_map/ppermute | solution.py:162
  697.4 76.3 %collective-permute-start.50 = (f32[1280,1280]{1,0:T(8,128)}, f32[1280,1280]{1,0:T(8,128)}, u32[]{:S(2)}, u32[]{:S(2)}) collective-permute-start(f32[1280,1280]{1,0:T(8,128)} %fusion.44), channel_id=1, source_target_pairs={{0,1},{1,0},{2,3},{3,2},{4,5},{5,4},{6,7},{7,6},{8,9},{9,8},{10,11... | collective-permute-start | bytes 19660808 | tf_op jit(solution)/shard_map/ppermute | solution.py:162
  745.4 56.4 %collective-permute-start.15 = (f32[320,1920]{1,0:T(8,128)}, f32[320,1920]{1,0:T(8,128)S(1)}, u32[]{:S(2)}, u32[]{:S(2)}) collective-permute-start(f32[320,1920]{1,0:T(8,128)} %dynamic-slice_add_fusion.4), channel_id=1, source_target_pairs={{0,2},{1,3},{2,0},{3,1},{4,6},{5,7},{6,4},{7,5},{8,10},{9,11},{10,... | collective-permute-start | bytes 7372808 | tf_op jit(solution)/shard_map/ppermute | solution.py:162
  746.5 108.0 %collective-permute-start.6 = (f32[320,1920]{1,0:T(8,128)}, f32[320,1920]{1,0:T(8,128)S(1)}, u32[]{:S(2)}, u32[]{:S(2)}) collective-permute-start(f32[320,1920]{1,0:T(8,128)} %dynamic-slice_add_fusion.5), channel_id=1, source_target_pairs={{0,2},{1,3},{2,0},{3,1},{4,6},{5,7},{6,4},{7,5},{8,10},{9,11},{10,... | collective-permute-start | bytes 7372808 | tf_op jit(solution)/shard_map/ppermute | solution.py:162
  756.4 101.9 %collective-permute-start.31 = (f32[160,1280]{1,0:T(8,128)S(1)}, f32[160,1280]{1,0:T(8,128)}, u32[]{:S(2)}, u32[]{:S(2)}) collective-permute-start(f32[160,1280]{1,0:T(8,128)S(1)} %pad_maximum_fusion.14), channel_id=1, source_target_pairs={{0,4},{4,0},{8,12},{12,8},{16,20},{20,16},{24,28},{28,24},{1,5},{5... | collective-permute-start | bytes 2457608 | tf_op jit(solution)/shard_map/ppermute | solution.py:162
  763.9 206.1 %collective-permute-start.42 = (f32[320,2560]{1,0:T(8,128)}, f32[320,2560]{1,0:T(8,128)S(1)}, u32[]{:S(2)}, u32[]{:S(2)}) collective-permute-start(f32[320,2560]{1,0:T(8,128)} %dynamic-slice_add_fusion.2), channel_id=1, source_target_pairs={{0,2},{1,3},{2,0},{3,1},{4,6},{5,7},{6,4},{7,5},{8,10},{9,11},{10,... | collective-permute-start | bytes 9830408 | tf_op jit(solution)/shard_map/ppermute | solution.py:162
  773.6 221.3 %collective-permute-start.33 = (f32[320,2560]{1,0:T(8,128)}, f32[320,2560]{1,0:T(8,128)S(1)}, u32[]{:S(2)}, u32[]{:S(2)}) collective-permute-start(f32[320,2560]{1,0:T(8,128)} %dynamic-slice_add_fusion.3), channel_id=1, source_target_pairs={{0,2},{1,3},{2,0},{3,1},{4,6},{5,7},{6,4},{7,5},{8,10},{9,11},{10,... | collective-permute-start | bytes 9830408 | tf_op jit(solution)/shard_map/ppermute | solution.py:162
  804.5 56.5 %collective-permute-start.16 = (f32[160,1920]{1,0:T(8,128)S(1)}, f32[160,1920]{1,0:T(8,128)S(1)}, u32[]{:S(2)}, u32[]{:S(2)}) collective-permute-start(f32[160,1920]{1,0:T(8,128)S(1)} %constant_dynamic-slice_fusion.25), channel_id=1, source_target_pairs={{0,4},{4,0},{8,12},{12,8},{16,20},{20,16},{24,28},{28,24},{1,5},{5... | collective-permute-start | bytes 3686408 | tf_op jit(solution)/shard_map/ppermute | solution.py:162
  960.9 104.3 %collective-permute-start.60 = (f32[640,1280]{1,0:T(8,128)S(1)}, f32[640,1280]{1,0:T(8,128)S(1)}, u32[]{:S(2)}, u32[]{:S(2)}) collective-permute-start(f32[640,1280]{1,0:T(8,128)S(1)} %dynamic-slice_add_fusion), channel_id=1, source_target_pairs={{0,2},{1,3},{2,0},{3,1},{4,6},{5,7},{6,4},{7,5},{8,10},{9,11},{10,... | collective-permute-start | bytes 9830408 | tf_op jit(solution)/shard_map/ppermute | solution.py:162
  962.3 170.7 %collective-permute-start.51 = (f32[640,1280]{1,0:T(8,128)}, f32[640,1280]{1,0:T(8,128)S(1)}, u32[]{:S(2)}, u32[]{:S(2)}) collective-permute-start(f32[640,1280]{1,0:T(8,128)} %dynamic-slice_add_fusion.1), channel_id=1, source_target_pairs={{0,2},{1,3},{2,0},{3,1},{4,6},{5,7},{6,4},{7,5},{8,10},{9,11},{10,... | collective-permute-start | bytes 9830408 | tf_op jit(solution)/shard_map/ppermute | solution.py:162
  967.3 171.1 %collective-permute-start.22 = (f32[160,1920]{1,0:T(8,128)}, f32[160,1920]{1,0:T(8,128)S(1)}, u32[]{:S(2)}, u32[]{:S(2)}) collective-permute-start(f32[160,1920]{1,0:T(8,128)} %pad_maximum_fusion.9), channel_id=1, source_target_pairs={{0,4},{4,0},{8,12},{12,8},{16,20},{20,16},{24,28},{28,24},{1,5},{5... | collective-permute-start | bytes 3686408 | tf_op jit(solution)/shard_map/ppermute | solution.py:162
  969.9 169.3 %collective-permute-start.13 = (f32[160,1920]{1,0:T(8,128)}, f32[160,1920]{1,0:T(8,128)}, u32[]{:S(2)}, u32[]{:S(2)}) collective-permute-start(f32[160,1920]{1,0:T(8,128)} %pad_maximum_fusion.8), channel_id=1, source_target_pairs={{0,4},{4,0},{8,12},{12,8},{16,20},{20,16},{24,28},{28,24},{1,5},{5... | collective-permute-start | bytes 3686408 | tf_op jit(solution)/shard_map/ppermute | solution.py:162
  994.9 148.4 %collective-permute-start.43 = (f32[160,2560]{1,0:T(8,128)}, f32[160,2560]{1,0:T(8,128)S(1)}, u32[]{:S(2)}, u32[]{:S(2)}) collective-permute-start(f32[160,2560]{1,0:T(8,128)} %constant_dynamic-slice_fusion.11), channel_id=1, source_target_pairs={{0,4},{4,0},{8,12},{12,8},{16,20},{20,16},{24,28},{28,24},{1,5},{5... | collective-permute-start | bytes 4915208 | tf_op jit(solution)/shard_map/ppermute | solution.py:162
  1065.2 80.3 %collective-permute-start.34 = (f32[160,2560]{1,0:T(8,128)}, f32[160,2560]{1,0:T(8,128)S(1)}, u32[]{:S(2)}, u32[]{:S(2)}) collective-permute-start(f32[160,2560]{1,0:T(8,128)} %constant_dynamic-slice_fusion.14), channel_id=1, source_target_pairs={{0,4},{4,0},{8,12},{12,8},{16,20},{20,16},{24,28},{28,24},{1,5},{5... | collective-permute-start | bytes 4915208 | tf_op jit(solution)/shard_map/ppermute | solution.py:162
  1133.0 38.9 %collective-permute-start.61 = (f32[320,1280]{1,0:T(8,128)}, f32[320,1280]{1,0:T(8,128)S(1)}, u32[]{:S(2)}, u32[]{:S(2)}) collective-permute-start(f32[320,1280]{1,0:T(8,128)} %constant_dynamic-slice_fusion), channel_id=1, source_target_pairs={{0,4},{4,0},{8,12},{12,8},{16,20},{20,16},{24,28},{28,24},{1,5},{5... | collective-permute-start | bytes 4915208 | tf_op jit(solution)/shard_map/ppermute | solution.py:162
  1138.4 65.6 %collective-permute-start.52 = (f32[320,1280]{1,0:T(8,128)}, f32[320,1280]{1,0:T(8,128)}, u32[]{:S(2)}, u32[]{:S(2)}) collective-permute-start(f32[320,1280]{1,0:T(8,128)} %constant_dynamic-slice_fusion.6), channel_id=1, source_target_pairs={{0,4},{4,0},{8,12},{12,8},{16,20},{20,16},{24,28},{28,24},{1,5},{5... | collective-permute-start | bytes 4915208 | tf_op jit(solution)/shard_map/ppermute | solution.py:162
  1143.6 64.5 %collective-permute-start.44 = (f32[80,2560]{1,0:T(8,128)S(1)}, f32[80,2560]{1,0:T(8,128)S(1)}, u32[]{:S(2)}, u32[]{:S(2)}) collective-permute-start(f32[80,2560]{1,0:T(8,128)S(1)} %constant_dynamic-slice_fusion.10), channel_id=1, source_target_pairs={{0,8},{4,12},{8,0},{12,4},{16,24},{20,28},{24,16},{28,20},{1,9},{5... | collective-permute-start | bytes 2457608 | tf_op jit(solution)/shard_map/ppermute | solution.py:162
  1145.7 63.2 %collective-permute-start.35 = (f32[80,2560]{1,0:T(8,128)S(1)}, f32[80,2560]{1,0:T(8,128)S(1)}, u32[]{:S(2)}, u32[]{:S(2)}) collective-permute-start(f32[80,2560]{1,0:T(8,128)S(1)} %constant_dynamic-slice_fusion.13), channel_id=1, source_target_pairs={{0,8},{4,12},{8,0},{12,4},{16,24},{20,28},{24,16},{28,20},{1,9},{5... | collective-permute-start | bytes 2457608 | tf_op jit(solution)/shard_map/ppermute | solution.py:162
  1172.2 39.3 %collective-permute-start.62 = (f32[160,1280]{1,0:T(8,128)S(1)}, f32[160,1280]{1,0:T(8,128)S(1)}, u32[]{:S(2)}, u32[]{:S(2)}) collective-permute-start(f32[160,1280]{1,0:T(8,128)S(1)} %constant_dynamic-slice_fusion.20), channel_id=1, source_target_pairs={{0,8},{4,12},{8,0},{12,4},{16,24},{20,28},{24,16},{28,20},{1,9},{5... | collective-permute-start | bytes 2457608 | tf_op jit(solution)/shard_map/ppermute | solution.py:162
  1209.1 74.0 %collective-permute-start.36 = (f32[40,2560]{1,0:T(8,128)S(1)}, f32[40,2560]{1,0:T(8,128)S(1)}, u32[]{:S(2)}, u32[]{:S(2)}) collective-permute-start(f32[40,2560]{1,0:T(8,128)S(1)} %constant_dynamic-slice_fusion.12), channel_id=1, source_target_pairs={{0,16},{4,20},{8,24},{12,28},{16,0},{20,4},{24,8},{28,12},{1,17},{... | collective-permute-start | bytes 1228808 | tf_op jit(solution)/shard_map/ppermute | solution.py:162
  1211.7 84.5 %collective-permute-start.63 = (f32[80,1280]{1,0:T(8,128)S(1)}, f32[80,1280]{1,0:T(8,128)S(1)}, u32[]{:S(2)}, u32[]{:S(2)}) collective-permute-start(f32[80,1280]{1,0:T(8,128)S(1)} %constant_dynamic-slice_fusion.1), channel_id=1, source_target_pairs={{0,16},{4,20},{8,24},{12,28},{16,0},{20,4},{24,8},{28,12},{1,17},{... | collective-permute-start | bytes 1228808 | tf_op jit(solution)/shard_map/ppermute | solution.py:162
  1240.6 73.2 %collective-permute-start.54 = (f32[80,1280]{1,0:T(8,128)S(1)}, f32[80,1280]{1,0:T(8,128)S(1)}, u32[]{:S(2)}, u32[]{:S(2)}) collective-permute-start(f32[80,1280]{1,0:T(8,128)S(1)} %constant_dynamic-slice_fusion.4), channel_id=1, source_target_pairs={{0,16},{4,20},{8,24},{12,28},{16,0},{20,4},{24,8},{28,12},{1,17},{... | collective-permute-start | bytes 1228808 | tf_op jit(solution)/shard_map/ppermute | solution.py:162
  1241.0 85.9 %collective-permute-start.47 = (f32[40,2560]{1,0:T(8,128)S(1)}, f32[40,2560]{1,0:T(8,128)S(1)}, u32[]{:S(2)}, u32[]{:S(2)}) collective-permute-start(f32[40,2560]{1,0:T(8,128)S(1)} %dynamic-slice_add_fusion.22), channel_id=1, source_target_pairs={{0,16},{4,20},{8,24},{12,28},{16,0},{20,4},{24,8},{28,12},{1,17},{... | collective-permute-start | bytes 1228808 | tf_op jit(solution)/shard_map/ppermute | solution.py:162
  1243.7 83.2 %collective-permute-start.48 = (f32[40,2560]{1,0:T(8,128)S(1)}, f32[40,2560]{1,0:T(8,128)S(1)}, u32[]{:S(2)}, u32[]{:S(2)}) collective-permute-start(f32[40,2560]{1,0:T(8,128)S(1)} %dynamic-slice_add_fusion.22), channel_id=1, source_target_pairs={{0,24},{4,28},{8,16},{12,20},{16,8},{20,12},{24,0},{28,4},{1,25},{... | collective-permute-start | bytes 1228808 | tf_op jit(solution)/shard_map/ppermute | solution.py:162
  1283.1 62.5 %collective-permute-start.46 = (f32[40,2560]{1,0:T(8,128)S(1)}, f32[40,2560]{1,0:T(8,128)S(1)}, u32[]{:S(2)}, u32[]{:S(2)}) collective-permute-start(f32[40,2560]{1,0:T(8,128)S(1)} %dynamic-slice_add_fusion.22), channel_id=1, source_target_pairs={{0,8},{4,12},{8,0},{12,4},{16,24},{20,28},{24,16},{28,20},{1,9},{5... | collective-permute-start | bytes 1228808 | tf_op jit(solution)/shard_map/ppermute | solution.py:162
  1296.2 65.8 %collective-permute-start.38 = (f32[40,2560]{1,0:T(8,128)S(1)}, f32[40,2560]{1,0:T(8,128)S(1)}, u32[]{:S(2)}, u32[]{:S(2)}) collective-permute-start(f32[40,2560]{1,0:T(8,128)S(1)} %dynamic-slice_add_fusion.23), channel_id=1, source_target_pairs={{0,16},{4,20},{8,24},{12,28},{16,0},{20,4},{24,8},{28,12},{1,17},{... | collective-permute-start | bytes 1228808 | tf_op jit(solution)/shard_map/ppermute | solution.py:162
  1313.8 48.3 %collective-permute-start.39 = (f32[40,2560]{1,0:T(8,128)S(1)}, f32[40,2560]{1,0:T(8,128)S(1)}, u32[]{:S(2)}, u32[]{:S(2)}) collective-permute-start(f32[40,2560]{1,0:T(8,128)S(1)} %dynamic-slice_add_fusion.23), channel_id=1, source_target_pairs={{0,24},{4,28},{8,16},{12,20},{16,8},{20,12},{24,0},{28,4},{1,25},{... | collective-permute-start | bytes 1228808 | tf_op jit(solution)/shard_map/ppermute | solution.py:162
  1326.9 53.7 %collective-permute-start.37 = (f32[40,2560]{1,0:T(8,128)S(1)}, f32[40,2560]{1,0:T(8,128)S(1)}, u32[]{:S(2)}, u32[]{:S(2)}) collective-permute-start(f32[40,2560]{1,0:T(8,128)S(1)} %dynamic-slice_add_fusion.23), channel_id=1, source_target_pairs={{0,8},{4,12},{8,0},{12,4},{16,24},{20,28},{24,16},{28,20},{1,9},{5... | collective-permute-start | bytes 1228808 | tf_op jit(solution)/shard_map/ppermute | solution.py:162
  1327.0 70.2 %collective-permute-start.65 = (f32[80,1280]{1,0:T(8,128)S(1)}, f32[80,1280]{1,0:T(8,128)S(1)}, u32[]{:S(2)}, u32[]{:S(2)}) collective-permute-start(f32[80,1280]{1,0:T(8,128)S(1)} %dynamic-slice_add_fusion.20), channel_id=1, source_target_pairs={{0,16},{4,20},{8,24},{12,28},{16,0},{20,4},{24,8},{28,12},{1,17},{... | collective-permute-start | bytes 1228808 | tf_op jit(solution)/shard_map/ppermute | solution.py:162
  1345.5 51.6 %collective-permute-start.66 = (f32[80,1280]{1,0:T(8,128)S(1)}, f32[80,1280]{1,0:T(8,128)S(1)}, u32[]{:S(2)}, u32[]{:S(2)}) collective-permute-start(f32[80,1280]{1,0:T(8,128)S(1)} %dynamic-slice_add_fusion.20), channel_id=1, source_target_pairs={{0,24},{4,28},{8,16},{12,20},{16,8},{20,12},{24,0},{28,4},{1,25},{... | collective-permute-start | bytes 1228808 | tf_op jit(solution)/shard_map/ppermute | solution.py:162
  1362.1 36.5 %collective-permute-start.64 = (f32[80,1280]{1,0:T(8,128)S(1)}, f32[80,1280]{1,0:T(8,128)S(1)}, u32[]{:S(2)}, u32[]{:S(2)}) collective-permute-start(f32[80,1280]{1,0:T(8,128)S(1)} %dynamic-slice_add_fusion.20), channel_id=1, source_target_pairs={{0,8},{4,12},{8,0},{12,4},{16,24},{20,28},{24,16},{28,20},{1,9},{5... | collective-permute-start | bytes 1228808 | tf_op jit(solution)/shard_map/ppermute | solution.py:162
  1362.1 52.7 %collective-permute-start.56 = (f32[80,1280]{1,0:T(8,128)S(1)}, f32[80,1280]{1,0:T(8,128)S(1)}, u32[]{:S(2)}, u32[]{:S(2)}) collective-permute-start(f32[80,1280]{1,0:T(8,128)S(1)} %dynamic-slice_add_fusion.21), channel_id=1, source_target_pairs={{0,16},{4,20},{8,24},{12,28},{16,0},{20,4},{24,8},{28,12},{1,17},{... | collective-permute-start | bytes 1228808 | tf_op jit(solution)/shard_map/ppermute | solution.py:162
  1380.6 35.5 %collective-permute-start.57 = (f32[80,1280]{1,0:T(8,128)S(1)}, f32[80,1280]{1,0:T(8,128)S(1)}, u32[]{:S(2)}, u32[]{:S(2)}) collective-permute-start(f32[80,1280]{1,0:T(8,128)S(1)} %dynamic-slice_add_fusion.21), channel_id=1, source_target_pairs={{0,24},{4,28},{8,16},{12,20},{16,8},{20,12},{24,0},{28,4},{1,25},{... | collective-permute-start | bytes 1228808 | tf_op jit(solution)/shard_map/ppermute | solution.py:162
  1397.2 38.7 %collective-permute-start.49 = (f32[160,2560]{1,0:T(8,128)S(1)}, f32[160,2560]{1,0:T(8,128)S(1)}, u32[]{:S(2)}, u32[]{:S(2)}) collective-permute-start(f32[160,2560]{1,0:T(8,128)S(1)} %pad_maximum_fusion.5), channel_id=1, source_target_pairs={{0,4},{4,0},{8,12},{12,8},{16,20},{20,16},{24,28},{28,24},{1,5},{5... | collective-permute-start | bytes 4915208 | tf_op jit(solution)/shard_map/ppermute | solution.py:162
  1398.6 107.7 %collective-permute-start.40 = (f32[160,2560]{1,0:T(8,128)S(1)}, f32[160,2560]{1,0:T(8,128)S(1)}, u32[]{:S(2)}, u32[]{:S(2)}) collective-permute-start(f32[160,2560]{1,0:T(8,128)S(1)} %pad_maximum_fusion.4), channel_id=1, source_target_pairs={{0,4},{4,0},{8,12},{12,8},{16,20},{20,16},{24,28},{28,24},{1,5},{5... | collective-permute-start | bytes 4915208 | tf_op jit(solution)/shard_map/ppermute | solution.py:162
  1414.8 91.3 %collective-permute-start.67 = (f32[320,1280]{1,0:T(8,128)S(1)}, f32[320,1280]{1,0:T(8,128)S(1)}, u32[]{:S(2)}, u32[]{:S(2)}) collective-permute-start(f32[320,1280]{1,0:T(8,128)S(1)} %pad_maximum_fusion.7), channel_id=1, source_target_pairs={{0,4},{4,0},{8,12},{12,8},{16,20},{20,16},{24,28},{28,24},{1,5},{5... | collective-permute-start | bytes 4915208 | tf_op jit(solution)/shard_map/ppermute | solution.py:162
  1416.5 107.9 %collective-permute-start.58 = (f32[320,1280]{1,0:T(8,128)S(1)}, f32[320,1280]{1,0:T(8,128)}, u32[]{:S(2)}, u32[]{:S(2)}) collective-permute-start(f32[320,1280]{1,0:T(8,128)S(1)} %pad_maximum_fusion.6), channel_id=1, source_target_pairs={{0,4},{4,0},{8,12},{12,8},{16,20},{20,16},{24,28},{28,24},{1,5},{5... | collective-permute-start | bytes 4915208 | tf_op jit(solution)/shard_map/ppermute | solution.py:162
  (94 other events, 1494.9 us)
Sparse Core Ops, SparseCore 0:
  9.5 70.1 all-gather.6
  81.3 29.2 all-gather.8
  112.1 85.0 all-gather.10
  198.6 85.0 all-gather.12

commit v2 on v1

--- a/solution.py
+++ b/solution.py
@@ -91,7 +91,7 @@
     d_v = jnp.where(low, dv_parts[0], dv_parts[1])
     d_q = (d_q * cos_tab - partner_lanes(d_q) * sin_tab) * HEAD_DIM ** -0.5
     d_k = d_k * cos_tab - partner_lanes(d_k) * sin_tab
-    pair = pl.program_id(1)
+    pair = pl.program_id(0)
     model_dim = dq_out.shape[2] // 3
     for i, grad in enumerate((d_q, d_k, d_v)):
         lanes = pl.ds(pl.multiple_of(pair * 128 + i * model_dim, 128), 128)
@@ -117,22 +117,32 @@
     )(qkv_proj, qkv_proj, qkv_proj, cos_tab, sin_tab, pad_row)
 
 
-def attention_bwd(q_val, k_val, v_val, d_ctx, cos_tab, sin_tab, pad_col):
+def attention_bwd(row, d_qkv, d_bias, q_val, k_val, v_val, d_ctx, cos_tab, sin_tab, pad_col):
     rows, seq, dim = q_val.shape
     pairs = dim // 128
-    blk = pl.BlockSpec((1, seq, 128), lambda b, p: (b, 0, p))
-    tab = pl.BlockSpec((seq, 128), lambda b, p: (0, 0))
+    blk = pl.BlockSpec((1, seq, 128), lambda p: (row, 0, p))
+    tab = pl.BlockSpec((seq, 128), lambda p: (0, 0))
+    operands = [q_val, k_val, v_val, d_ctx, cos_tab, sin_tab, pad_col]
+    in_specs = [blk] * 4 + [tab, tab, pl.BlockSpec((1, seq, 128), lambda p: (row, 0, 0))]
+    kernel, aliases = attn_bwd_kernel, {}
+    if d_qkv is not None:
+        def kernel(*refs):
+            attn_bwd_kernel(*refs[:7], *refs[9:])
+
+        operands += [d_qkv, d_bias]
+        in_specs += [pl.BlockSpec(memory_space=pl.ANY)] * 2
+        aliases = {7: 0, 8: 1}
     return pl.pallas_call(
-        attn_bwd_kernel, grid=(rows, pairs),
-        in_specs=[blk] * 4 + [tab, tab, pl.BlockSpec((1, seq, 128), lambda b, p: (b, 0, 0))],
-        out_specs=[pl.BlockSpec((1, seq, 3 * dim), lambda b, p: (b, 0, 0)),
-                   pl.BlockSpec((1, 8, 3 * dim), lambda b, p: (b, 0, 0))],
+        kernel, grid=(pairs,), in_specs=in_specs,
+        out_specs=[pl.BlockSpec((1, seq, 3 * dim), lambda p: (row, 0, 0)),
+                   pl.BlockSpec((1, 8, 3 * dim), lambda p: (row, 0, 0))],
         out_shape=[jax.ShapeDtypeStruct((rows, seq, 3 * dim), BF16),
                    jax.ShapeDtypeStruct((rows, 8, 3 * dim), F32)],
-        cost_estimate=pl.CostEstimate(flops=int(6e10), bytes_accessed=rows * seq * dim * 14,
-                                      transcendentals=rows * seq * seq * 2 * pairs),
+        input_output_aliases=aliases,
+        cost_estimate=pl.CostEstimate(flops=int(2e10), bytes_accessed=seq * dim * 14,
+                                      transcendentals=seq * seq * 2 * pairs),
         name='attn_bwd',
-    )(q_val, k_val, v_val, d_ctx, cos_tab, sin_tab, pad_col)
+    )(*operands)
 
 
 def fc1_kernel(x_ref, w_ref, bias_ref, act_ref, slope_ref):
@@ -277,8 +287,10 @@
         d_mid_b16 = d_mid.astype(BF16)
         d_ctx = dot_f32(d_mid_b16, w_out, 1, 1).astype(BF16)
         got_out = send_half(place, context, d_mid_b16)
-        d_qkv, g_b_qkv = attention_bwd(queries, key_rows, values, d_ctx.reshape(batch, seq, dim),
-                                       cos_tab, sin_tab, jnp.broadcast_to(pad_f32[:, :, None], (batch, seq, 128)))
+        d_qkv = g_b_qkv = None
+        for b in range(batch):
+            d_qkv, g_b_qkv = attention_bwd(
+                b, d_qkv, g_b_qkv, queries, key_rows, values, d_ctx.reshape(batch, seq, dim), cos_tab, sin_tab, jnp.broadcast_to(pad_f32[:, :, None], (batch, seq, 128)))
         sums_out = own_half(place, got_out, context, d_mid_b16)
         d_qkv = d_qkv.reshape(rows, 3 * dim)
         g_b_qkv = jnp.sum(g_b_qkv, axis=(0, 1))

time: 1560 us -> 1570 us (level)
    pallas_call x1 -> x3, Pallas kernels: 75.3 us -> 81.2 us  [attention_bwd(): pl.pallas_call(kernel, grid=(pairs,), in_specs=in_specs, out_specs=[pl.Bl...]
where the time goes in v2:
time: 1570 us; the launch traced here: 1540 us
  waiting for transfers between devices  743 us (47%)
  matrix products  299 us (19%)
  Pallas kernels  182 us (12%)
  starting transfers between devices  122 us (8%)
  other arithmetic  81.5 us (5%)
  local copies, waits for them, and re-layouts  72.2 us (5%)
  blocking collectives  25.3 us (2%)
  between operations  17.2 us (1%)
    ppermute x68, waiting for transfers between devices, swap(): return lax.ppermute(x_val, axis, [(i, i ^ mask) for i in range(size)])  660 us
    dot_general x30, matrix products, dot_f32(): lax.dot_general(lhs, rhs, (((lhs_dim,), (rhs_dim,)), ((), ())), preferred...  299 us
    ppermute x68, starting transfers between devices, swap(): return lax.ppermute(x_val, axis, [(i, i ^ mask) for i in range(size)])  122 us
    pallas_call x3, Pallas kernels, attention_bwd(): pl.pallas_call(kernel, grid=(pairs,), in_specs=in_specs, out_specs=[pl.Bl...  81.2 us
    all_gather x4, waiting for transfers between devices, local_step(): lax.all_gather(w, 'fsdp', axis=0, tiled=True)  80.6 us
    pallas_call x1, Pallas kernels, fc1_gelu(): pl.pallas_call(fc1_kernel, grid=(width // tile_n, rows // tile_m), in_spe...  52.8 us
    pallas_call x1, Pallas kernels, attention_fwd(): pl.pallas_call(attn_fwd_kernel, grid=(rows, pairs), in_specs=[blk(0), blk...  48.2 us
  transfers between devices with their start and end apart: 72, of which 36 were waited for; matrix products, arithmetic and copies ran while one was open for 18% of the time, Pallas kernels for 7%

profile of v2, /device:TPU:0, one launch (start us, length us, event | category | flops | bytes accessed | tf_op | source)
XLA Modules:
  0.0 1542.0 jit_solution(1487361741980379357)
XLA Ops:
  14.0 13.7 all-reduce.7
  55.4 24.3 %all-gather.7.cloned.1.call-done = bf16[1280,3840]{1,0:T(8,128)(2,1)} async-done(((bf16[320,3840]{1,0:T(8,128)(2,1)}), bf16[1280,3840]{1,0:T(8,128)(2,1)}) %all-gather.7.cloned.1.call-update) | async-done | bytes 9830416 | tf_op jit(solution)/shard_map/all_gather | solution.py:247
  79.7 22.2 %convolution_add_fusion = f32[1536,3840]{1,0:T(8,128)} fusion(bf16[1536,1280]{1,0:T(8,128)(2,1)} %copy-done.14, bf16[1280,3840]{1,0:T(8,128)(2,1)} %all-gather.7.cloned.1.call-done, f32[3840]{0:T(1024)S(1)} %convert_element_type.90), kind=kOutput, calls=%fused_computation.1 | convolution fusion | flops 15105392640 | bytes 37370880 | tf_op jit(solution)/shard_map/dot_general | solution.py:20
  102.5 48.2 %attn_fwd.1 = (bf16[3,512,1280]{2,1,0:T(8,128)(2,1)}, bf16[3,512,1280]{2,1,0:T(8,128)(2,1)}, bf16[3,512,1280]{2,1,0:T(8,128)(2,1)}, bf16[3,512,1280]{2,1,0:T(8,128)(2,1)}) custom-call(f32[3,512,3840]{2,1,0:T(8,128)} %bitcast.80, f32[3,512,3840]{2,1,0:T(8,128)} %bitcast.81, f32[3,512,3840]{2,1,0:T(8,128)} %bitcast.82, ...), custom_call_target="tpu_custom_call" | custom-call | flops 30000001024 | bytes 39321600 | tf_op jit(solution)/shard_map/attn_fwd/pallas_call | solution.py:109
  150.7 9.3 fusion.130
  173.9 23.3 %all-gather.11.cloned.1.call-done.w_ref = bf16[1280,5120]{1,0:T(8,128)(2,1)} async-done(((bf16[320,5120]{1,0:T(8,128)(2,1)}), bf16[1280,5120]{1,0:T(8,128)(2,1)}) %all-gather.11.cloned.1.call-update) | async-done | bytes 13107216 | tf_op jit(solution)/shard_map/all_gather | solution.py:247
  197.9 52.8 %fc1_gelu.1 = (bf16[1536,5120]{1,0:T(8,128)(2,1)}, f32[1536,5120]{1,0:T(8,128)}) custom-call(bf16[1536,1280]{1,0:T(8,128)(2,1)} %copy-done.11, bf16[1280,5120]{1,0:T(8,128)(2,1)} %all-gather.11.cloned.1.call-done.w_ref, f32[8,5120]{1,0:T(8,128)} %broadcast_in_dim.21.bias_ref), custom_call_target="tpu_custom_call" | custom-call | flops 20132659200 | bytes 47185920 | tf_op jit(solution)/shard_map/fc1_gelu/pallas_call | solution.py:159
  250.7 33.0 %all-gather.13.cloned.1.call-done = bf16[5120,1280]{1,0:T(8,128)(2,1)} async-done(((bf16[1280,1280]{1,0:T(8,128)(2,1)}), bf16[5120,1280]{1,0:T(8,128)(2,1)}) %all-gather.13.cloned.1.call-update) | async-done | bytes 13107216 | tf_op jit(solution)/shard_map/all_gather | solution.py:247
  283.7 29.5 %fusion.128 = (f32[5120]{0:T(1024)}, bf16[1536,5120]{1,0:T(8,128)(2,1)}) fusion(f32[1536,5120]{1,0:T(8,128)} %get-tuple-element.28, bf16[1536,1280]{1,0:T(8,128)(2,1)} %bitcast.60, bf16[5120,1280]{1,0:T(8,128)(2,1)} %all-gather.13.cloned.1.call-done), kind=kOutput, calls=%fused_computation.269 | convolution fusion | flops 20156248064 | bytes 64245760 | tf_op jit(solution)/shard_map/dot_general | solution.py:20
  313.2 30.1 %fusion.132 = (f32[1280]{0:T(1024)}, f32[1536,1280]{0,1:T(8,128)}) fusion(bf16[1536,5120]{1,0:T(8,128)(2,1)} %get-tuple-element.58, bf16[1280,5120]{1,0:T(8,128)(2,1)} %all-gather.11.cloned.1.call-done.w_ref), kind=kOutput, calls=%fused_computation.273 | convolution fusion | flops 20134623232 | bytes 36705280 | tf_op jit(solution)/shard_map/dot_general | solution.py:20
  343.3 9.2 copy.51
  379.3 27.1 %attn_bwd.3 = (bf16[3,512,3840]{2,1,0:T(8,128)(2,1)}, f32[3,8,3840]{2,1,0:T(8,128)}) custom-call(bf16[3,512,1280]{2,1,0:T(8,128)(2,1)} %get-tuple-element.29.q_in.refs_0_, bf16[3,512,1280]{2,1,0:T(8,128)(2,1)} %get-tuple-element.30.k_in.refs_1_, bf16[3,512,1280]{2,1,0:T(8,128)(2,1)} %get-tuple-element.31.v_in.refs_2_, bf16[3,512,1280]{2,1,0:T(8,128)(2,1)} %bitcast.91, ...), custom_call_target="tpu_custom_call" | custom-call | flops 20000000000 | bytes 9175040 | tf_op jit(solution)/shard_map/attn_bwd/pallas_call | solution.py:135
  406.4 27.0 %attn_bwd.4 = (bf16[3,512,3840]{2,1,0:T(8,128)(2,1)}, f32[3,8,3840]{2,1,0:T(8,128)}) custom-call(bf16[3,512,1280]{2,1,0:T(8,128)(2,1)} %get-tuple-element.29.q_in.refs_0_, bf16[3,512,1280]{2,1,0:T(8,128)(2,1)} %get-tuple-element.30.k_in.refs_1_, bf16[3,512,1280]{2,1,0:T(8,128)(2,1)} %get-tuple-element.31.v_in.refs_2_, ...), custom_call_target="tpu_custom_call", output_to_operand_aliasing={{0}: (7, {}), {1}: (8, {})} | custom-call | flops 20000000000 | bytes 9175040 | tf_op jit(solution)/shard_map/attn_bwd/pallas_call | solution.py:135
  433.4 27.2 %attn_bwd.5 = (bf16[3,512,3840]{2,1,0:T(8,128)(2,1)}, f32[3,8,3840]{2,1,0:T(8,128)}) custom-call(bf16[3,512,1280]{2,1,0:T(8,128)(2,1)} %get-tuple-element.29.q_in.refs_0_, bf16[3,512,1280]{2,1,0:T(8,128)(2,1)} %get-tuple-element.30.k_in.refs_1_, bf16[3,512,1280]{2,1,0:T(8,128)(2,1)} %get-tuple-element.31.v_in.refs_2_, ...), custom_call_target="tpu_custom_call", output_to_operand_aliasing={{0}: (7, {}), {1}: (8, {})} | custom-call | flops 20000000000 | bytes 9175040 | tf_op jit(solution)/shard_map/attn_bwd/pallas_call | solution.py:135
  460.6 9.5 fusion.34
  476.5 17.6 %fusion.131 = (f32[1280]{0:T(1024)S(1)}, f32[1536,1280]{0,1:T(8,128)}) fusion(bf16[1536,3840]{1,0:T(8,128)(2,1)S(1)} %bitcast.89, bf16[1280,3840]{1,0:T(8,128)(2,1)S(1)} %bitcast.79), kind=kOutput, calls=%fused_computation.272 | convolution fusion | flops 15101459456 | bytes 29496320 | tf_op jit(solution)/shard_map/dot_general | solution.py:20
  494.1 9.2 copy.52
  545.6 26.5 %fusion.19 = bf16[1536,1280]{1,0:T(8,128)(2,1)} fusion(f32[1536,1280]{1,0:T(8,128)} %copy-done, bf16[1536,5120]{1,0:T(8,128)(2,1)S(1)} %bitcast.69, bf16[5120,1280]{1,0:T(8,128)(2,1)} %all-gather.13.cloned.1.call-done, f32[1280]{0:T(1024)S(1)} %copy-done.51), kind=kOutput, calls=%fused_computation.32 | convolution fusion | flops 20138557440 | bytes 40637440 | tf_op jit(solution)/shard_map/dot_general | solution.py:20
  572.2 10.4 fusion.48
  582.5 10.0 fusion.22
  592.5 10.5 fusion.28
  628.3 19.0 %collective-permute-done.24 = f32[320,1280]{1,0:T(8,128)} collective-permute-done((f32[320,1280]{1,0:T(8,128)}, f32[320,1280]{1,0:T(8,128)}, u32[]{:S(2)}, u32[]{:S(2)}) %collective-permute-start.24) | collective-permute-done | bytes 1638432 | tf_op jit(solution)/shard_map/ppermute | solution.py:172
  655.9 13.2 collective-permute-done.2
  721.5 12.2 collective-permute-done.29
  787.9 20.0 %collective-permute-done.15 = f32[320,1920]{1,0:T(8,128)S(1)} collective-permute-done((f32[320,1920]{1,0:T(8,128)}, f32[320,1920]{1,0:T(8,128)S(1)}, u32[]{:S(2)}, u32[]{:S(2)}) %collective-permute-start.15) | collective-permute-done | bytes 2457632 | tf_op jit(solution)/shard_map/ppermute | solution.py:172
  811.9 48.5 %collective-permute-done.6 = f32[320,1920]{1,0:T(8,128)S(1)} collective-permute-done((f32[320,1920]{1,0:T(8,128)}, f32[320,1920]{1,0:T(8,128)S(1)}, u32[]{:S(2)}, u32[]{:S(2)}) %collective-permute-start.6) | collective-permute-done | bytes 2457632 | tf_op jit(solution)/shard_map/ppermute | solution.py:172
  868.3 19.1 %collective-permute-done.7 = f32[160,1920]{1,0:T(8,128)S(1)} collective-permute-done((f32[160,1920]{1,0:T(8,128)S(1)}, f32[160,1920]{1,0:T(8,128)S(1)}, u32[]{:S(2)}, u32[]{:S(2)}) %collective-permute-start.7) | collective-permute-done | bytes 1228832 | tf_op jit(solution)/shard_map/ppermute | solution.py:172
  890.6 15.9 %collective-permute-done.8 = f32[80,1920]{1,0:T(8,128)S(1)} collective-permute-done((f32[80,1920]{1,0:T(8,128)S(1)}, f32[80,1920]{1,0:T(8,128)S(1)}, u32[]{:S(2)}, u32[]{:S(2)}) %collective-permute-start.8) | collective-permute-done | bytes 614432 | tf_op jit(solution)/shard_map/ppermute | solution.py:172
  911.1 22.6 %collective-permute-done.9 = f32[40,1920]{1,0:T(8,128)S(1)} collective-permute-done((f32[40,1920]{1,0:T(8,128)S(1)}, f32[40,1920]{1,0:T(8,128)S(1)}, u32[]{:S(2)}, u32[]{:S(2)}) %collective-permute-start.9) | collective-permute-done | bytes 307232 | tf_op jit(solution)/shard_map/ppermute | solution.py:172
  946.8 15.6 %collective-permute-start.10 = (f32[40,1920]{1,0:T(8,128)S(1)}, f32[40,1920]{1,0:T(8,128)S(1)}, u32[]{:S(2)}, u32[]{:S(2)}) collective-permute-start(f32[40,1920]{1,0:T(8,128)S(1)} %dynamic-slice_add_fusion.26), channel_id=1, source_target_pairs={{0,8},{4,12},{8,0},{12,4},{16,24},{20,28},{24,16},{28,20},{1,9},{5... | collective-permute-start | bytes 921608 | tf_op jit(solution)/shard_map/ppermute | solution.py:172
  980.8 20.1 %collective-permute-done.33 = f32[320,2560]{1,0:T(8,128)S(1)} collective-permute-done((f32[320,2560]{1,0:T(8,128)}, f32[320,2560]{1,0:T(8,128)S(1)}, u32[]{:S(2)}, u32[]{:S(2)}) %collective-permute-start.33) | collective-permute-done | bytes 3276832 | tf_op jit(solution)/shard_map/ppermute | solution.py:172
  1006.8 64.3 %collective-permute-done.60 = f32[640,1280]{1,0:T(8,128)S(1)} collective-permute-done((f32[640,1280]{1,0:T(8,128)S(1)}, f32[640,1280]{1,0:T(8,128)S(1)}, u32[]{:S(2)}, u32[]{:S(2)}) %collective-permute-start.60) | collective-permute-done | bytes 3276832 | tf_op jit(solution)/shard_map/ppermute | solution.py:172
  1076.6 62.5 %collective-permute-done.51 = f32[640,1280]{1,0:T(8,128)S(1)} collective-permute-done((f32[640,1280]{1,0:T(8,128)}, f32[640,1280]{1,0:T(8,128)S(1)}, u32[]{:S(2)}, u32[]{:S(2)}) %collective-permute-start.51) | collective-permute-done | bytes 3276832 | tf_op jit(solution)/shard_map/ppermute | solution.py:172
  1152.0 25.9 %collective-permute-done.61 = f32[320,1280]{1,0:T(8,128)S(1)} collective-permute-done((f32[320,1280]{1,0:T(8,128)}, f32[320,1280]{1,0:T(8,128)S(1)}, u32[]{:S(2)}, u32[]{:S(2)}) %collective-permute-start.61) | collective-permute-done | bytes 1638432 | tf_op jit(solution)/shard_map/ppermute | solution.py:172
  1180.0 30.0 %collective-permute-done.52 = f32[320,1280]{1,0:T(8,128)} collective-permute-done((f32[320,1280]{1,0:T(8,128)}, f32[320,1280]{1,0:T(8,128)}, u32[]{:S(2)}, u32[]{:S(2)}) %collective-permute-start.52) | collective-permute-done | bytes 1638432 | tf_op jit(solution)/shard_map/ppermute | solution.py:172
  1218.2 28.1 %collective-permute-done.53 = f32[160,1280]{1,0:T(8,128)S(1)} collective-permute-done((f32[160,1280]{1,0:T(8,128)S(1)}, f32[160,1280]{1,0:T(8,128)S(1)}, u32[]{:S(2)}, u32[]{:S(2)}) %collective-permute-start.53) | collective-permute-done | bytes 819232 | tf_op jit(solution)/shard_map/ppermute | solution.py:172
  1251.9 37.1 %collective-permute-done.36 = f32[40,2560]{1,0:T(8,128)S(1)} collective-permute-done((f32[40,2560]{1,0:T(8,128)S(1)}, f32[40,2560]{1,0:T(8,128)S(1)}, u32[]{:S(2)}, u32[]{:S(2)}) %collective-permute-start.36) | collective-permute-done | bytes 409632 | tf_op jit(solution)/shard_map/ppermute | solution.py:172
  1289.1 13.1 collective-permute-done.63
  1302.2 17.5 %collective-permute-done.54 = f32[80,1280]{1,0:T(8,128)S(1)} collective-permute-done((f32[80,1280]{1,0:T(8,128)S(1)}, f32[80,1280]{1,0:T(8,128)S(1)}, u32[]{:S(2)}, u32[]{:S(2)}) %collective-permute-start.54) | collective-permute-done | bytes 409632 | tf_op jit(solution)/shard_map/ppermute | solution.py:172
  1321.7 11.2 collective-permute-done.47
  1332.9 18.5 %collective-permute-start.65 = (f32[80,1280]{1,0:T(8,128)S(1)}, f32[80,1280]{1,0:T(8,128)S(1)}, u32[]{:S(2)}, u32[]{:S(2)}) collective-permute-start(f32[80,1280]{1,0:T(8,128)S(1)} %dynamic-slice_add_fusion.20), channel_id=1, source_target_pairs={{0,16},{4,20},{8,24},{12,28},{16,0},{20,4},{24,8},{28,12},{1,17},{... | collective-permute-start | bytes 1228808 | tf_op jit(solution)/shard_map/ppermute | solution.py:172
  1353.6 14.4 collective-permute-done.38
  1368.0 18.5 %collective-permute-start.56 = (f32[80,1280]{1,0:T(8,128)S(1)}, f32[80,1280]{1,0:T(8,128)S(1)}, u32[]{:S(2)}, u32[]{:S(2)}) collective-permute-start(f32[80,1280]{1,0:T(8,128)S(1)} %dynamic-slice_add_fusion.21), channel_id=1, source_target_pairs={{0,16},{4,20},{8,24},{12,28},{16,0},{20,4},{24,8},{28,12},{1,17},{... | collective-permute-start | bytes 1228808 | tf_op jit(solution)/shard_map/ppermute | solution.py:172
  1389.0 14.2 collective-permute-done.65
  1405.5 15.2 collective-permute-done.56
  1423.1 18.7 %collective-permute-done.49 = f32[160,2560]{1,0:T(8,128)S(1)} collective-permute-done((f32[160,2560]{1,0:T(8,128)S(1)}, f32[160,2560]{1,0:T(8,128)S(1)}, u32[]{:S(2)}, u32[]{:S(2)}) %collective-permute-start.49) | collective-permute-done | bytes 1638432 | tf_op jit(solution)/shard_map/ppermute | solution.py:172
  1442.1 69.9 %collective-permute-done.67 = f32[320,1280]{1,0:T(8,128)S(1)} collective-permute-done((f32[320,1280]{1,0:T(8,128)S(1)}, f32[320,1280]{1,0:T(8,128)S(1)}, u32[]{:S(2)}, u32[]{:S(2)}) %collective-permute-start.67) | collective-permute-done | bytes 1638432 | tf_op jit(solution)/shard_map/ppermute | solution.py:172
  1515.9 14.4 collective-permute-done.58
  (441 shorter events, 374.5 us)
Async XLA Ops:
  7.2 72.5 %all-gather.7.cloned.1.call-start = ((), (), s32[]{:S(2)}) async-start(), calls=%async_computation | async-start | bytes 12288000 | tf_op jit(solution)/shard_map/all_gather | solution.py:247
  7.9 142.8 %all-gather.9.cloned.1.call-start = ((), (), s32[]{:S(2)}) async-start(), calls=%async_computation.1 | async-start | bytes 4096000 | tf_op jit(solution)/shard_map/all_gather | solution.py:247
  8.8 188.4 %all-gather.11.cloned.1.call-start = ((), (), s32[]{:S(2)}) async-start(), calls=%async_computation.2 | async-start | bytes 16384000 | tf_op jit(solution)/shard_map/all_gather | solution.py:247
  9.5 274.2 %all-gather.13.cloned.1.call-start = ((), (), s32[]{:S(2)}) async-start(), calls=%async_computation.3 | async-start | bytes 16384000 | tf_op jit(solution)/shard_map/all_gather | solution.py:247
  530.6 95.1 %collective-permute-start = (f32[2,115,128]{2,1,0:T(8,128)}, f32[2,115,128]{2,1,0:T(8,128)}, u32[]{:S(2)}, u32[]{:S(2)}) collective-permute-start(f32[2,115,128]{2,1,0:T(8,128)} %dynamic-slice_bitcast_fusion), channel_id=1, source_target_pairs={{0,1},{1,0},{2,3},{3,2},{4,5},{5,4},{6,7},{7,6},{8,9},{9,8},{10,11... | collective-permute-start | bytes 353288 | tf_op jit(solution)/shard_map/ppermute | solution.py:172
  530.9 159.0 %collective-permute-start.14 = (f32[640,1920]{1,0:T(8,128)}, f32[640,1920]{1,0:T(8,128)}, u32[]{:S(2)}, u32[]{:S(2)}) collective-permute-start(f32[640,1920]{1,0:T(8,128)} %fusion.34), channel_id=1, source_target_pairs={{0,1},{1,0},{2,3},{3,2},{4,5},{5,4},{6,7},{7,6},{8,9},{9,8},{10,11... | collective-permute-start | bytes 14745608 | tf_op jit(solution)/shard_map/ppermute | solution.py:172
  531.1 189.7 %collective-permute-start.5 = (f32[640,1920]{1,0:T(8,128)}, f32[640,1920]{1,0:T(8,128)}, u32[]{:S(2)}, u32[]{:S(2)}) collective-permute-start(f32[640,1920]{1,0:T(8,128)} %fusion.40), channel_id=1, source_target_pairs={{0,1},{1,0},{2,3},{3,2},{4,5},{5,4},{6,7},{7,6},{8,9},{9,8},{10,11... | collective-permute-start | bytes 14745608 | tf_op jit(solution)/shard_map/ppermute | solution.py:172
  538.4 64.6 %collective-permute-start.23 = (f32[640,1280]{1,0:T(8,128)}, f32[640,1280]{1,0:T(8,128)S(1)}, u32[]{:S(2)}, u32[]{:S(2)}) collective-permute-start(f32[640,1280]{1,0:T(8,128)} %fusion.52), channel_id=1, source_target_pairs={{0,1},{1,0},{2,3},{3,2},{4,5},{5,4},{6,7},{7,6},{8,9},{9,8},{10,11... | collective-permute-start | bytes 9830408 | tf_op jit(solution)/shard_map/ppermute | solution.py:172
  608.6 38.7 %collective-permute-start.24 = (f32[320,1280]{1,0:T(8,128)}, f32[320,1280]{1,0:T(8,128)}, u32[]{:S(2)}, u32[]{:S(2)}) collective-permute-start(f32[320,1280]{1,0:T(8,128)} %dynamic-slice_add_fusion.10), channel_id=1, source_target_pairs={{0,2},{1,3},{2,0},{3,1},{4,6},{5,7},{6,4},{7,5},{8,10},{9,11},{10,... | collective-permute-start | bytes 4915208 | tf_op jit(solution)/shard_map/ppermute | solution.py:172
  625.6 126.9 %collective-permute-start.41 = (f32[640,2560]{1,0:T(8,128)}, f32[640,2560]{1,0:T(8,128)}, u32[]{:S(2)}, u32[]{:S(2)}) collective-permute-start(f32[640,2560]{1,0:T(8,128)} %fusion.22), channel_id=1, source_target_pairs={{0,1},{1,0},{2,3},{3,2},{4,5},{5,4},{6,7},{7,6},{8,9},{9,8},{10,11... | collective-permute-start | bytes 19660808 | tf_op jit(solution)/shard_map/ppermute | solution.py:172
  669.1 93.3 %collective-permute-start.59 = (f32[1280,1280]{1,0:T(8,128)}, f32[1280,1280]{1,0:T(8,128)}, u32[]{:S(2)}, u32[]{:S(2)}) collective-permute-start(f32[1280,1280]{1,0:T(8,128)} %fusion.48), channel_id=1, source_target_pairs={{0,1},{1,0},{2,3},{3,2},{4,5},{5,4},{6,7},{7,6},{8,9},{9,8},{10,11... | collective-permute-start | bytes 19660808 | tf_op jit(solution)/shard_map/ppermute | solution.py:172
  689.8 80.1 %collective-permute-start.32 = (f32[640,2560]{1,0:T(8,128)}, f32[640,2560]{1,0:T(8,128)}, u32[]{:S(2)}, u32[]{:S(2)}) collective-permute-start(f32[640,2560]{1,0:T(8,128)} %fusion.28), channel_id=1, source_target_pairs={{0,1},{1,0},{2,3},{3,2},{4,5},{5,4},{6,7},{7,6},{8,9},{9,8},{10,11... | collective-permute-start | bytes 19660808 | tf_op jit(solution)/shard_map/ppermute | solution.py:172
  703.3 76.3 %collective-permute-start.50 = (f32[1280,1280]{1,0:T(8,128)}, f32[1280,1280]{1,0:T(8,128)}, u32[]{:S(2)}, u32[]{:S(2)}) collective-permute-start(f32[1280,1280]{1,0:T(8,128)} %fusion.44), channel_id=1, source_target_pairs={{0,1},{1,0},{2,3},{3,2},{4,5},{5,4},{6,7},{7,6},{8,9},{9,8},{10,11... | collective-permute-start | bytes 19660808 | tf_op jit(solution)/shard_map/ppermute | solution.py:172
  751.4 56.4 %collective-permute-start.15 = (f32[320,1920]{1,0:T(8,128)}, f32[320,1920]{1,0:T(8,128)S(1)}, u32[]{:S(2)}, u32[]{:S(2)}) collective-permute-start(f32[320,1920]{1,0:T(8,128)} %dynamic-slice_add_fusion.4), channel_id=1, source_target_pairs={{0,2},{1,3},{2,0},{3,1},{4,6},{5,7},{6,4},{7,5},{8,10},{9,11},{10,... | collective-permute-start | bytes 7372808 | tf_op jit(solution)/shard_map/ppermute | solution.py:172
  752.5 108.0 %collective-permute-start.6 = (f32[320,1920]{1,0:T(8,128)}, f32[320,1920]{1,0:T(8,128)S(1)}, u32[]{:S(2)}, u32[]{:S(2)}) collective-permute-start(f32[320,1920]{1,0:T(8,128)} %dynamic-slice_add_fusion.5), channel_id=1, source_target_pairs={{0,2},{1,3},{2,0},{3,1},{4,6},{5,7},{6,4},{7,5},{8,10},{9,11},{10,... | collective-permute-start | bytes 7372808 | tf_op jit(solution)/shard_map/ppermute | solution.py:172
  762.4 102.0 %collective-permute-start.31 = (f32[160,1280]{1,0:T(8,128)S(1)}, f32[160,1280]{1,0:T(8,128)}, u32[]{:S(2)}, u32[]{:S(2)}) collective-permute-start(f32[160,1280]{1,0:T(8,128)S(1)} %pad_maximum_fusion.14), channel_id=1, source_target_pairs={{0,4},{4,0},{8,12},{12,8},{16,20},{20,16},{24,28},{28,24},{1,5},{5... | collective-permute-start | bytes 2457608 | tf_op jit(solution)/shard_map/ppermute | solution.py:172
  769.9 206.0 %collective-permute-start.42 = (f32[320,2560]{1,0:T(8,128)}, f32[320,2560]{1,0:T(8,128)S(1)}, u32[]{:S(2)}, u32[]{:S(2)}) collective-permute-start(f32[320,2560]{1,0:T(8,128)} %dynamic-slice_add_fusion.2), channel_id=1, source_target_pairs={{0,2},{1,3},{2,0},{3,1},{4,6},{5,7},{6,4},{7,5},{8,10},{9,11},{10,... | collective-permute-start | bytes 9830408 | tf_op jit(solution)/shard_map/ppermute | solution.py:172
  779.7 221.3 %collective-permute-start.33 = (f32[320,2560]{1,0:T(8,128)}, f32[320,2560]{1,0:T(8,128)S(1)}, u32[]{:S(2)}, u32[]{:S(2)}) collective-permute-start(f32[320,2560]{1,0:T(8,128)} %dynamic-slice_add_fusion.3), channel_id=1, source_target_pairs={{0,2},{1,3},{2,0},{3,1},{4,6},{5,7},{6,4},{7,5},{8,10},{9,11},{10,... | collective-permute-start | bytes 9830408 | tf_op jit(solution)/shard_map/ppermute | solution.py:172
  810.5 56.5 %collective-permute-start.16 = (f32[160,1920]{1,0:T(8,128)S(1)}, f32[160,1920]{1,0:T(8,128)S(1)}, u32[]{:S(2)}, u32[]{:S(2)}) collective-permute-start(f32[160,1920]{1,0:T(8,128)S(1)} %constant_dynamic-slice_fusion.25), channel_id=1, source_target_pairs={{0,4},{4,0},{8,12},{12,8},{16,20},{20,16},{24,28},{28,24},{1,5},{5... | collective-permute-start | bytes 3686408 | tf_op jit(solution)/shard_map/ppermute | solution.py:172
  966.7 104.4 %collective-permute-start.60 = (f32[640,1280]{1,0:T(8,128)S(1)}, f32[640,1280]{1,0:T(8,128)S(1)}, u32[]{:S(2)}, u32[]{:S(2)}) collective-permute-start(f32[640,1280]{1,0:T(8,128)S(1)} %dynamic-slice_add_fusion), channel_id=1, source_target_pairs={{0,2},{1,3},{2,0},{3,1},{4,6},{5,7},{6,4},{7,5},{8,10},{9,11},{10,... | collective-permute-start | bytes 9830408 | tf_op jit(solution)/shard_map/ppermute | solution.py:172
  968.4 170.7 %collective-permute-start.51 = (f32[640,1280]{1,0:T(8,128)}, f32[640,1280]{1,0:T(8,128)S(1)}, u32[]{:S(2)}, u32[]{:S(2)}) collective-permute-start(f32[640,1280]{1,0:T(8,128)} %dynamic-slice_add_fusion.1), channel_id=1, source_target_pairs={{0,2},{1,3},{2,0},{3,1},{4,6},{5,7},{6,4},{7,5},{8,10},{9,11},{10,... | collective-permute-start | bytes 9830408 | tf_op jit(solution)/shard_map/ppermute | solution.py:172
  973.2 171.2 %collective-permute-start.22 = (f32[160,1920]{1,0:T(8,128)}, f32[160,1920]{1,0:T(8,128)S(1)}, u32[]{:S(2)}, u32[]{:S(2)}) collective-permute-start(f32[160,1920]{1,0:T(8,128)} %pad_maximum_fusion.9), channel_id=1, source_target_pairs={{0,4},{4,0},{8,12},{12,8},{16,20},{20,16},{24,28},{28,24},{1,5},{5... | collective-permute-start | bytes 3686408 | tf_op jit(solution)/shard_map/ppermute | solution.py:172
  975.9 169.3 %collective-permute-start.13 = (f32[160,1920]{1,0:T(8,128)}, f32[160,1920]{1,0:T(8,128)}, u32[]{:S(2)}, u32[]{:S(2)}) collective-permute-start(f32[160,1920]{1,0:T(8,128)} %pad_maximum_fusion.8), channel_id=1, source_target_pairs={{0,4},{4,0},{8,12},{12,8},{16,20},{20,16},{24,28},{28,24},{1,5},{5... | collective-permute-start | bytes 3686408 | tf_op jit(solution)/shard_map/ppermute | solution.py:172
  1000.9 148.4 %collective-permute-start.43 = (f32[160,2560]{1,0:T(8,128)}, f32[160,2560]{1,0:T(8,128)S(1)}, u32[]{:S(2)}, u32[]{:S(2)}) collective-permute-start(f32[160,2560]{1,0:T(8,128)} %constant_dynamic-slice_fusion.11), channel_id=1, source_target_pairs={{0,4},{4,0},{8,12},{12,8},{16,20},{20,16},{24,28},{28,24},{1,5},{5... | collective-permute-start | bytes 4915208 | tf_op jit(solution)/shard_map/ppermute | solution.py:172
  1071.1 80.3 %collective-permute-start.34 = (f32[160,2560]{1,0:T(8,128)}, f32[160,2560]{1,0:T(8,128)S(1)}, u32[]{:S(2)}, u32[]{:S(2)}) collective-permute-start(f32[160,2560]{1,0:T(8,128)} %constant_dynamic-slice_fusion.14), channel_id=1, source_target_pairs={{0,4},{4,0},{8,12},{12,8},{16,20},{20,16},{24,28},{28,24},{1,5},{5... | collective-permute-start | bytes 4915208 | tf_op jit(solution)/shard_map/ppermute | solution.py:172
  1139.0 38.9 %collective-permute-start.61 = (f32[320,1280]{1,0:T(8,128)}, f32[320,1280]{1,0:T(8,128)S(1)}, u32[]{:S(2)}, u32[]{:S(2)}) collective-permute-start(f32[320,1280]{1,0:T(8,128)} %constant_dynamic-slice_fusion), channel_id=1, source_target_pairs={{0,4},{4,0},{8,12},{12,8},{16,20},{20,16},{24,28},{28,24},{1,5},{5... | collective-permute-start | bytes 4915208 | tf_op jit(solution)/shard_map/ppermute | solution.py:172
  1144.4 65.6 %collective-permute-start.52 = (f32[320,1280]{1,0:T(8,128)}, f32[320,1280]{1,0:T(8,128)}, u32[]{:S(2)}, u32[]{:S(2)}) collective-permute-start(f32[320,1280]{1,0:T(8,128)} %constant_dynamic-slice_fusion.6), channel_id=1, source_target_pairs={{0,4},{4,0},{8,12},{12,8},{16,20},{20,16},{24,28},{28,24},{1,5},{5... | collective-permute-start | bytes 4915208 | tf_op jit(solution)/shard_map/ppermute | solution.py:172
  1149.6 64.5 %collective-permute-start.44 = (f32[80,2560]{1,0:T(8,128)S(1)}, f32[80,2560]{1,0:T(8,128)S(1)}, u32[]{:S(2)}, u32[]{:S(2)}) collective-permute-start(f32[80,2560]{1,0:T(8,128)S(1)} %constant_dynamic-slice_fusion.10), channel_id=1, source_target_pairs={{0,8},{4,12},{8,0},{12,4},{16,24},{20,28},{24,16},{28,20},{1,9},{5... | collective-permute-start | bytes 2457608 | tf_op jit(solution)/shard_map/ppermute | solution.py:172
  1151.7 63.1 %collective-permute-start.35 = (f32[80,2560]{1,0:T(8,128)S(1)}, f32[80,2560]{1,0:T(8,128)S(1)}, u32[]{:S(2)}, u32[]{:S(2)}) collective-permute-start(f32[80,2560]{1,0:T(8,128)S(1)} %constant_dynamic-slice_fusion.13), channel_id=1, source_target_pairs={{0,8},{4,12},{8,0},{12,4},{16,24},{20,28},{24,16},{28,20},{1,9},{5... | collective-permute-start | bytes 2457608 | tf_op jit(solution)/shard_map/ppermute | solution.py:172
  1178.2 39.3 %collective-permute-start.62 = (f32[160,1280]{1,0:T(8,128)S(1)}, f32[160,1280]{1,0:T(8,128)S(1)}, u32[]{:S(2)}, u32[]{:S(2)}) collective-permute-start(f32[160,1280]{1,0:T(8,128)S(1)} %constant_dynamic-slice_fusion.20), channel_id=1, source_target_pairs={{0,8},{4,12},{8,0},{12,4},{16,24},{20,28},{24,16},{28,20},{1,9},{5... | collective-permute-start | bytes 2457608 | tf_op jit(solution)/shard_map/ppermute | solution.py:172
  1215.0 74.0 %collective-permute-start.36 = (f32[40,2560]{1,0:T(8,128)S(1)}, f32[40,2560]{1,0:T(8,128)S(1)}, u32[]{:S(2)}, u32[]{:S(2)}) collective-permute-start(f32[40,2560]{1,0:T(8,128)S(1)} %constant_dynamic-slice_fusion.12), channel_id=1, source_target_pairs={{0,16},{4,20},{8,24},{12,28},{16,0},{20,4},{24,8},{28,12},{1,17},{... | collective-permute-start | bytes 1228808 | tf_op jit(solution)/shard_map/ppermute | solution.py:172
  1217.7 84.5 %collective-permute-start.63 = (f32[80,1280]{1,0:T(8,128)S(1)}, f32[80,1280]{1,0:T(8,128)S(1)}, u32[]{:S(2)}, u32[]{:S(2)}) collective-permute-start(f32[80,1280]{1,0:T(8,128)S(1)} %constant_dynamic-slice_fusion.1), channel_id=1, source_target_pairs={{0,16},{4,20},{8,24},{12,28},{16,0},{20,4},{24,8},{28,12},{1,17},{... | collective-permute-start | bytes 1228808 | tf_op jit(solution)/shard_map/ppermute | solution.py:172
  1246.5 73.3 %collective-permute-start.54 = (f32[80,1280]{1,0:T(8,128)S(1)}, f32[80,1280]{1,0:T(8,128)S(1)}, u32[]{:S(2)}, u32[]{:S(2)}) collective-permute-start(f32[80,1280]{1,0:T(8,128)S(1)} %constant_dynamic-slice_fusion.4), channel_id=1, source_target_pairs={{0,16},{4,20},{8,24},{12,28},{16,0},{20,4},{24,8},{28,12},{1,17},{... | collective-permute-start | bytes 1228808 | tf_op jit(solution)/shard_map/ppermute | solution.py:172
  1247.0 85.9 %collective-permute-start.47 = (f32[40,2560]{1,0:T(8,128)S(1)}, f32[40,2560]{1,0:T(8,128)S(1)}, u32[]{:S(2)}, u32[]{:S(2)}) collective-permute-start(f32[40,2560]{1,0:T(8,128)S(1)} %dynamic-slice_add_fusion.22), channel_id=1, source_target_pairs={{0,16},{4,20},{8,24},{12,28},{16,0},{20,4},{24,8},{28,12},{1,17},{... | collective-permute-start | bytes 1228808 | tf_op jit(solution)/shard_map/ppermute | solution.py:172
  1249.6 83.3 %collective-permute-start.48 = (f32[40,2560]{1,0:T(8,128)S(1)}, f32[40,2560]{1,0:T(8,128)S(1)}, u32[]{:S(2)}, u32[]{:S(2)}) collective-permute-start(f32[40,2560]{1,0:T(8,128)S(1)} %dynamic-slice_add_fusion.22), channel_id=1, source_target_pairs={{0,24},{4,28},{8,16},{12,20},{16,8},{20,12},{24,0},{28,4},{1,25},{... | collective-permute-start | bytes 1228808 | tf_op jit(solution)/shard_map/ppermute | solution.py:172
  1289.0 62.4 %collective-permute-start.46 = (f32[40,2560]{1,0:T(8,128)S(1)}, f32[40,2560]{1,0:T(8,128)S(1)}, u32[]{:S(2)}, u32[]{:S(2)}) collective-permute-start(f32[40,2560]{1,0:T(8,128)S(1)} %dynamic-slice_add_fusion.22), channel_id=1, source_target_pairs={{0,8},{4,12},{8,0},{12,4},{16,24},{20,28},{24,16},{28,20},{1,9},{5... | collective-permute-start | bytes 1228808 | tf_op jit(solution)/shard_map/ppermute | solution.py:172
  1302.2 65.8 %collective-permute-start.38 = (f32[40,2560]{1,0:T(8,128)S(1)}, f32[40,2560]{1,0:T(8,128)S(1)}, u32[]{:S(2)}, u32[]{:S(2)}) collective-permute-start(f32[40,2560]{1,0:T(8,128)S(1)} %dynamic-slice_add_fusion.23), channel_id=1, source_target_pairs={{0,16},{4,20},{8,24},{12,28},{16,0},{20,4},{24,8},{28,12},{1,17},{... | collective-permute-start | bytes 1228808 | tf_op jit(solution)/shard_map/ppermute | solution.py:172
  1319.7 48.3 %collective-permute-start.39 = (f32[40,2560]{1,0:T(8,128)S(1)}, f32[40,2560]{1,0:T(8,128)S(1)}, u32[]{:S(2)}, u32[]{:S(2)}) collective-permute-start(f32[40,2560]{1,0:T(8,128)S(1)} %dynamic-slice_add_fusion.23), channel_id=1, source_target_pairs={{0,24},{4,28},{8,16},{12,20},{16,8},{20,12},{24,0},{28,4},{1,25},{... | collective-permute-start | bytes 1228808 | tf_op jit(solution)/shard_map/ppermute | solution.py:172
  1332.9 53.7 %collective-permute-start.37 = (f32[40,2560]{1,0:T(8,128)S(1)}, f32[40,2560]{1,0:T(8,128)S(1)}, u32[]{:S(2)}, u32[]{:S(2)}) collective-permute-start(f32[40,2560]{1,0:T(8,128)S(1)} %dynamic-slice_add_fusion.23), channel_id=1, source_target_pairs={{0,8},{4,12},{8,0},{12,4},{16,24},{20,28},{24,16},{28,20},{1,9},{5... | collective-permute-start | bytes 1228808 | tf_op jit(solution)/shard_map/ppermute | solution.py:172
  1332.9 70.2 %collective-permute-start.65 = (f32[80,1280]{1,0:T(8,128)S(1)}, f32[80,1280]{1,0:T(8,128)S(1)}, u32[]{:S(2)}, u32[]{:S(2)}) collective-permute-start(f32[80,1280]{1,0:T(8,128)S(1)} %dynamic-slice_add_fusion.20), channel_id=1, source_target_pairs={{0,16},{4,20},{8,24},{12,28},{16,0},{20,4},{24,8},{28,12},{1,17},{... | collective-permute-start | bytes 1228808 | tf_op jit(solution)/shard_map/ppermute | solution.py:172
  1351.5 51.7 %collective-permute-start.66 = (f32[80,1280]{1,0:T(8,128)S(1)}, f32[80,1280]{1,0:T(8,128)S(1)}, u32[]{:S(2)}, u32[]{:S(2)}) collective-permute-start(f32[80,1280]{1,0:T(8,128)S(1)} %dynamic-slice_add_fusion.20), channel_id=1, source_target_pairs={{0,24},{4,28},{8,16},{12,20},{16,8},{20,12},{24,0},{28,4},{1,25},{... | collective-permute-start | bytes 1228808 | tf_op jit(solution)/shard_map/ppermute | solution.py:172
  1368.0 36.5 %collective-permute-start.64 = (f32[80,1280]{1,0:T(8,128)S(1)}, f32[80,1280]{1,0:T(8,128)S(1)}, u32[]{:S(2)}, u32[]{:S(2)}) collective-permute-start(f32[80,1280]{1,0:T(8,128)S(1)} %dynamic-slice_add_fusion.20), channel_id=1, source_target_pairs={{0,8},{4,12},{8,0},{12,4},{16,24},{20,28},{24,16},{28,20},{1,9},{5... | collective-permute-start | bytes 1228808 | tf_op jit(solution)/shard_map/ppermute | solution.py:172
  1368.0 52.7 %collective-permute-start.56 = (f32[80,1280]{1,0:T(8,128)S(1)}, f32[80,1280]{1,0:T(8,128)S(1)}, u32[]{:S(2)}, u32[]{:S(2)}) collective-permute-start(f32[80,1280]{1,0:T(8,128)S(1)} %dynamic-slice_add_fusion.21), channel_id=1, source_target_pairs={{0,16},{4,20},{8,24},{12,28},{16,0},{20,4},{24,8},{28,12},{1,17},{... | collective-permute-start | bytes 1228808 | tf_op jit(solution)/shard_map/ppermute | solution.py:172
  1386.6 35.6 %collective-permute-start.57 = (f32[80,1280]{1,0:T(8,128)S(1)}, f32[80,1280]{1,0:T(8,128)S(1)}, u32[]{:S(2)}, u32[]{:S(2)}) collective-permute-start(f32[80,1280]{1,0:T(8,128)S(1)} %dynamic-slice_add_fusion.21), channel_id=1, source_target_pairs={{0,24},{4,28},{8,16},{12,20},{16,8},{20,12},{24,0},{28,4},{1,25},{... | collective-permute-start | bytes 1228808 | tf_op jit(solution)/shard_map/ppermute | solution.py:172
  1403.1 38.7 %collective-permute-start.49 = (f32[160,2560]{1,0:T(8,128)S(1)}, f32[160,2560]{1,0:T(8,128)S(1)}, u32[]{:S(2)}, u32[]{:S(2)}) collective-permute-start(f32[160,2560]{1,0:T(8,128)S(1)} %pad_maximum_fusion.5), channel_id=1, source_target_pairs={{0,4},{4,0},{8,12},{12,8},{16,20},{20,16},{24,28},{28,24},{1,5},{5... | collective-permute-start | bytes 4915208 | tf_op jit(solution)/shard_map/ppermute | solution.py:172
  1404.6 107.7 %collective-permute-start.40 = (f32[160,2560]{1,0:T(8,128)S(1)}, f32[160,2560]{1,0:T(8,128)S(1)}, u32[]{:S(2)}, u32[]{:S(2)}) collective-permute-start(f32[160,2560]{1,0:T(8,128)S(1)} %pad_maximum_fusion.4), channel_id=1, source_target_pairs={{0,4},{4,0},{8,12},{12,8},{16,20},{20,16},{24,28},{28,24},{1,5},{5... | collective-permute-start | bytes 4915208 | tf_op jit(solution)/shard_map/ppermute | solution.py:172
  1420.7 91.3 %collective-permute-start.67 = (f32[320,1280]{1,0:T(8,128)S(1)}, f32[320,1280]{1,0:T(8,128)S(1)}, u32[]{:S(2)}, u32[]{:S(2)}) collective-permute-start(f32[320,1280]{1,0:T(8,128)S(1)} %pad_maximum_fusion.7), channel_id=1, source_target_pairs={{0,4},{4,0},{8,12},{12,8},{16,20},{20,16},{24,28},{28,24},{1,5},{5... | collective-permute-start | bytes 4915208 | tf_op jit(solution)/shard_map/ppermute | solution.py:172
  1422.5 107.9 %collective-permute-start.58 = (f32[320,1280]{1,0:T(8,128)S(1)}, f32[320,1280]{1,0:T(8,128)}, u32[]{:S(2)}, u32[]{:S(2)}) collective-permute-start(f32[320,1280]{1,0:T(8,128)S(1)} %pad_maximum_fusion.6), channel_id=1, source_target_pairs={{0,4},{4,0},{8,12},{12,8},{16,20},{20,16},{24,28},{28,24},{1,5},{5... | collective-permute-start | bytes 4915208 | tf_op jit(solution)/shard_map/ppermute | solution.py:172
  (94 other events, 1399.4 us)
Sparse Core Ops, SparseCore 0:
  9.5 70.1 all-gather.6
  81.3 29.2 all-gather.8
  112.1 85.0 all-gather.10
  198.6 85.0 all-gather.12
